TPU v7x, 32 devices: a whole 2x2x4 slice. The times are simulated.
32 devices in a mesh: dp: 2 (over x), tp: 4 (over z), cp: 4 (over y, core).
Axes of the slice: x: 2, y: 2, z: 4, core: 2. Of those that a mesh axis runs over, the one named last changes fastest.
Arguments:
- x: bfloat16 [4096, 2048], P(('dp', 'cp')), parts along dimension 0
- doc_id: int32 [4096], P(('dp', 'cp')), parts along dimension 0
- pos_in_doc: int32 [4096], P(('dp', 'cp')), parts along dimension 0
- norm_gain: float32 [2048], replicated
- w_q: bfloat16 [2048, 2048], P(None, 'tp')
- w_k: bfloat16 [2048, 512], P(None, 'tp')
- w_v: bfloat16 [2048, 512], P(None, 'tp')
- w_o: bfloat16 [2048, 2048], P('tp')
- inv_freq: float32 [32], replicated
Outputs:
- output 1: bfloat16 [4096, 2048], P(('dp', 'cp')), parts along dimension 0
- output 2: bfloat16 [4096, 8, 64], P(('dp', 'cp'), 'tp'), parts along dimension 0
- output 3: bfloat16 [4096, 8, 64], P(('dp', 'cp'), 'tp'), parts along dimension 0
There are 2 independent parts. A program takes and returns all parts, laid end to end along the dimension named above; an argument that names none is the same for every part.
All inputs are finite; a program needn't handle non-finite values.
Results may differ from a plain program's by a relative error of at most 0.00417696.
Values are sent between devices in bfloat16 or wider.
A program may use at most 1 GiB of HBM per device.

v0:
```python
import jax
import jax.numpy as jnp
from jax import lax
from jax.sharding import PartitionSpec as P

QUERY_ROWS = 128


def rms_norm(x_in, norm_gain):
    x_f32 = x_in.astype(jnp.float32)
    inv_rms = lax.rsqrt(jnp.mean(x_f32 * x_f32, axis=-1, keepdims=True) + 1e-5)
    return (x_f32 * inv_rms * norm_gain).astype(jnp.bfloat16)


def apply_rope(vectors, cos_t, sin_t):
    half_dim = vectors.shape[-1] // 2
    lower_half = vectors[..., :half_dim].astype(jnp.float32)
    upper_half = vectors[..., half_dim:].astype(jnp.float32)
    turned = jnp.concatenate([lower_half * cos_t - upper_half * sin_t, upper_half * cos_t + lower_half * sin_t], axis=-1)
    return turned.astype(jnp.bfloat16)


def project(x_in, pos_in_doc, norm_gain, w_q, w_k, w_v, inv_freq):
    num_rows = x_in.shape[0]
    head_dim = 2 * inv_freq.shape[0]
    kv_heads = w_k.shape[1] // head_dim
    group_size = w_q.shape[1] // (head_dim * kv_heads)
    normed = rms_norm(x_in, norm_gain)
    q_new = jnp.dot(normed, w_q, preferred_element_type=jnp.float32).astype(jnp.bfloat16).reshape(num_rows, kv_heads, group_size, head_dim)
    k_new = jnp.dot(normed, w_k, preferred_element_type=jnp.float32).astype(jnp.bfloat16).reshape(num_rows, kv_heads, head_dim)
    v_new = jnp.dot(normed, w_v, preferred_element_type=jnp.float32).astype(jnp.bfloat16).reshape(num_rows, kv_heads, head_dim)
    rope_angle = pos_in_doc.astype(jnp.float32)[:, None] * inv_freq[None, :]
    cos_t = jnp.cos(rope_angle)
    sin_t = jnp.sin(rope_angle)
    q_rot = apply_rope(q_new, cos_t[:, None, None, :], sin_t[:, None, None, :])
    k_rot = apply_rope(k_new, cos_t[:, None, :], sin_t[:, None, :])
    return q_rot, k_rot, v_new


def global_index(stored_pos, local_rows, cp_size):
    piece_len = local_rows // 2
    owner = stored_pos // local_rows
    within = stored_pos % local_rows
    piece_id = jnp.where(within < piece_len, owner, 2 * cp_size - 1 - owner)
    return piece_id * piece_len + within % piece_len


def attention(q_rot, key_rows, val_rows, q_doc, q_idx, key_doc, key_idx):
    local_rows, kv_heads, group_size, head_dim = q_rot.shape
    blocks = local_rows // QUERY_ROWS
    score_scale = head_dim ** -0.5

    def attend(block_args):
        q_blk, doc_blk, idx_blk = block_args
        scores = jnp.einsum('qngd,knd->ngqk', q_blk, key_rows, preferred_element_type=jnp.float32) * score_scale
        visible = (doc_blk[:, None] == key_doc[None, :]) & (key_idx[None, :] <= idx_blk[:, None])
        scores = jnp.where(visible, scores, -1e30)
        attn_probs = jax.nn.softmax(scores, axis=-1).astype(jnp.bfloat16)
        return jnp.einsum('ngqk,knd->qngd', attn_probs, val_rows, preferred_element_type=jnp.float32).astype(jnp.bfloat16)

    attn_out = lax.map(attend, (q_rot.reshape(blocks, QUERY_ROWS, kv_heads, group_size, head_dim), q_doc.reshape(blocks, QUERY_ROWS), q_idx.reshape(blocks, QUERY_ROWS)))
    return attn_out.reshape(local_rows, kv_heads * group_size * head_dim)


def solution(mesh):
    cp_size = mesh.shape['cp']

    def local_step(x_in, doc_id, pos_in_doc, norm_gain, w_q, w_k, w_v, w_o, inv_freq):
        local_rows = x_in.shape[0]
        tokens = local_rows * cp_size
        q_rot, k_rot, v_new = project(x_in, pos_in_doc, norm_gain, w_q, w_k, w_v, inv_freq)
        k_all = lax.all_gather(k_rot, 'cp', tiled=True)
        v_all = lax.all_gather(v_new, 'cp', tiled=True)
        doc_all = lax.all_gather(doc_id, 'cp', tiled=True)
        cp_index = lax.axis_index('cp')
        q_idx = global_index(cp_index * local_rows + jnp.arange(local_rows), local_rows, cp_size)
        key_idx = global_index(jnp.arange(tokens), local_rows, cp_size)
        attn_out = attention(q_rot, k_all, v_all, doc_id, q_idx, doc_all, key_idx)
        part_sum = jnp.dot(attn_out, w_o, preferred_element_type=jnp.float32)
        full_sum = lax.psum(part_sum, 'tp')
        y_out = (x_in.astype(jnp.float32) + full_sum).astype(jnp.bfloat16)
        return y_out, k_rot, v_new

    row_spec = P(('dp', 'cp'))
    in_specs = (P(('dp', 'cp'), None), row_spec, row_spec, P(), P(None, 'tp'), P(None, 'tp'), P(None, 'tp'), P('tp', None), P())
    out_specs = (P(('dp', 'cp'), None), P(('dp', 'cp'), 'tp', None), P(('dp', 'cp'), 'tp', None))
    return jax.shard_map(local_step, mesh=mesh, in_specs=in_specs, out_specs=out_specs, check_vma=False)
```

profile of v0, /device:TPU:0, one launch (start us, length us, event | category | flops | bytes accessed | tf_op | source)
XLA Modules:
  0.0 265.5 jit_solution(9336800424771040000)
XLA Ops:
  7.3 2.2 fusion.51
  9.5 0.8 convert_element_type.50
  10.3 1.0 multiply_cosine_fusion
  11.2 2.6 convolution_convert_fusion.2
  13.9 8.7 %all_gather.10 = bf16[2048,2,64]{0,2,1:T(8,128)(2,1)S(1)} all-gather(bf16[512,2,64]{0,2,1:T(8,128)(2,1)S(1)} %pad_maximum_fusion.1), channel_id=1, replica_groups=mesh['dp'=2,'tp'=4,'cp'=4] {'cp'}, dimensions={0}, use_global_device_ids=true | all-gather | bytes 655360 | tf_op jit(solution)/shard_map/all_gather | solution.py:72
  22.6 1.4 convolution_convert_fusion
  24.4 0.3 pad_maximum_fusion
  24.8 1.0 copy.14
  25.7 2.6 convolution_convert_fusion.1
  28.4 7.3 %all_gather.11 = bf16[2048,2,64]{0,2,1:T(8,128)(2,1)S(1)} all-gather(bf16[512,2,64]{0,2,1:T(8,128)(2,1)S(1)} %bitcast.92), channel_id=1, replica_groups=mesh['dp'=2,'tp'=4,'cp'=4] {'cp'}, dimensions={0}, use_global_device_ids=true | all-gather | bytes 655360 | tf_op jit(solution)/shard_map/all_gather | solution.py:73
  35.6 5.3 %all-gather = s32[4,1,512]{2,1,0:T(1,128)S(1)} all-gather(s32[1,1,512]{2,1,0:T(1,128)S(1)} %bitcast.95), channel_id=1, replica_groups=mesh['dp'=2,'tp'=4,'cp'=4] {'cp'}, dimensions={0}, use_global_device_ids=true | all-gather | bytes 10240 | tf_op jit(solution)/shard_map/all_gather | solution.py:74
  41.0 53.2 %while.11 = (s32[]{:T(128)}, bf16[4,128,2,4,64]{1,4,3,2,0:T(8,128)(2,1)}, s32[4,128]{1,0:T(4,128)S(1)}, s32[2048]{0:T(1024)S(1)}, s32[4,128]{1,0:T(4,128)S(1)}, ...) while((s32[]{:T(128)}, ...), condition=%wide.region_4.5_spmd.clone, body=%wide.region_1.4_spmd.clone.sunk | while | flops 550365184 | bytes 18649184 | solution.py:61
  41.3 7.5 %fusion.99 = (f32[2,4,128]{2,1,0:T(4,128)}, f32[2,4,128,2048]{3,2,1,0:T(8,128)}) fusion(pred[128,2048]{1,0:T(8,128)(4,1)S(1)} %compare_and_fusion.2, bf16[2048,2,64]{0,2,1:T(8,128)(2,1)S(1)} %get-tuple-element.192, bf16[4,128,2,4,64]{1,4,3,2,0:T(8,128)(2,1)} %get-tuple-element.191, s32[]{:T(128)} %get-tuple-element.177), kind=kOutput, calls=%fused_computation.102.clone.1 | convolution fusion | flops 276826112 | bytes 9310720 | tf_op jit(solution)/shard_map/while/body/eval_jaxpr/sub | solution.py:58
  48.8 5.5 %fusion.100 = bf16[4,128,2,4,64]{1,4,3,2,0:T(8,128)(2,1)} fusion(bf16[4,128,2,4,64]{1,4,3,2,0:T(8,128)(2,1)} %get-tuple-element.178, s32[]{:T(128)} %get-tuple-element.177, f32[2,4,128,2048]{3,2,1,0:T(8,128)} %get-tuple-element.166, f32[2,4,128]{2,1,0:T(4,128)} %get-tuple-element.167, bf16[2048,2,64]{0,2,1:T(8,128)(2,1)S(1)} %get-tuple-element.193), kind=kOutput, calls=%fused_computation.14.clone.1 | convolution fusion | flops 272695296 | bytes 9048576 | tf_op jit(solution)/shard_map/while/body/eval_jaxpr/ngqk,knd->qngd/dot_general | solution.py:59
  54.6 7.5 %fusion.99 = (f32[2,4,128]{2,1,0:T(4,128)}, f32[2,4,128,2048]{3,2,1,0:T(8,128)}) fusion(pred[128,2048]{1,0:T(8,128)(4,1)S(1)} %compare_and_fusion.2, bf16[2048,2,64]{0,2,1:T(8,128)(2,1)S(1)} %get-tuple-element.192, bf16[4,128,2,4,64]{1,4,3,2,0:T(8,128)(2,1)} %get-tuple-element.191, s32[]{:T(128)} %get-tuple-element.177), kind=kOutput, calls=%fused_computation.102.clone.1 | convolution fusion | flops 276826112 | bytes 9310720 | tf_op jit(solution)/shard_map/while/body/eval_jaxpr/sub | solution.py:58
  62.1 5.5 %fusion.100 = bf16[4,128,2,4,64]{1,4,3,2,0:T(8,128)(2,1)} fusion(bf16[4,128,2,4,64]{1,4,3,2,0:T(8,128)(2,1)} %get-tuple-element.178, s32[]{:T(128)} %get-tuple-element.177, f32[2,4,128,2048]{3,2,1,0:T(8,128)} %get-tuple-element.166, f32[2,4,128]{2,1,0:T(4,128)} %get-tuple-element.167, bf16[2048,2,64]{0,2,1:T(8,128)(2,1)S(1)} %get-tuple-element.193), kind=kOutput, calls=%fused_computation.14.clone.1 | convolution fusion | flops 272695296 | bytes 9048576 | tf_op jit(solution)/shard_map/while/body/eval_jaxpr/ngqk,knd->qngd/dot_general | solution.py:59
  67.9 7.5 %fusion.99 = (f32[2,4,128]{2,1,0:T(4,128)}, f32[2,4,128,2048]{3,2,1,0:T(8,128)}) fusion(pred[128,2048]{1,0:T(8,128)(4,1)S(1)} %compare_and_fusion.2, bf16[2048,2,64]{0,2,1:T(8,128)(2,1)S(1)} %get-tuple-element.192, bf16[4,128,2,4,64]{1,4,3,2,0:T(8,128)(2,1)} %get-tuple-element.191, s32[]{:T(128)} %get-tuple-element.177), kind=kOutput, calls=%fused_computation.102.clone.1 | convolution fusion | flops 276826112 | bytes 9310720 | tf_op jit(solution)/shard_map/while/body/eval_jaxpr/sub | solution.py:58
  75.4 5.5 %fusion.100 = bf16[4,128,2,4,64]{1,4,3,2,0:T(8,128)(2,1)} fusion(bf16[4,128,2,4,64]{1,4,3,2,0:T(8,128)(2,1)} %get-tuple-element.178, s32[]{:T(128)} %get-tuple-element.177, f32[2,4,128,2048]{3,2,1,0:T(8,128)} %get-tuple-element.166, f32[2,4,128]{2,1,0:T(4,128)} %get-tuple-element.167, bf16[2048,2,64]{0,2,1:T(8,128)(2,1)S(1)} %get-tuple-element.193), kind=kOutput, calls=%fused_computation.14.clone.1 | convolution fusion | flops 272695296 | bytes 9048576 | tf_op jit(solution)/shard_map/while/body/eval_jaxpr/ngqk,knd->qngd/dot_general | solution.py:59
  81.2 7.5 %fusion.99 = (f32[2,4,128]{2,1,0:T(4,128)}, f32[2,4,128,2048]{3,2,1,0:T(8,128)}) fusion(pred[128,2048]{1,0:T(8,128)(4,1)S(1)} %compare_and_fusion.2, bf16[2048,2,64]{0,2,1:T(8,128)(2,1)S(1)} %get-tuple-element.192, bf16[4,128,2,4,64]{1,4,3,2,0:T(8,128)(2,1)} %get-tuple-element.191, s32[]{:T(128)} %get-tuple-element.177), kind=kOutput, calls=%fused_computation.102.clone.1 | convolution fusion | flops 276826112 | bytes 9310720 | tf_op jit(solution)/shard_map/while/body/eval_jaxpr/sub | solution.py:58
  88.7 5.5 %fusion.100 = bf16[4,128,2,4,64]{1,4,3,2,0:T(8,128)(2,1)} fusion(bf16[4,128,2,4,64]{1,4,3,2,0:T(8,128)(2,1)} %get-tuple-element.178, s32[]{:T(128)} %get-tuple-element.177, f32[2,4,128,2048]{3,2,1,0:T(8,128)} %get-tuple-element.166, f32[2,4,128]{2,1,0:T(4,128)} %get-tuple-element.167, bf16[2048,2,64]{0,2,1:T(8,128)(2,1)S(1)} %get-tuple-element.193), kind=kOutput, calls=%fused_computation.14.clone.1 | convolution fusion | flops 272695296 | bytes 9048576 | tf_op jit(solution)/shard_map/while/body/eval_jaxpr/ngqk,knd->qngd/dot_general | solution.py:59
  94.2 1.5 copy.15
  95.7 3.2 %fusion.59 = f32[512,2048]{1,0:T(8,128)} fusion(bf16[512,2048]{1,0:T(8,128)(2,1)S(1)} %copy-done, bf16[64,8,4,128]{3,2,1,0:T(4,128)(2,1)S(1)} %bitcast.89), kind=kOutput, calls=%fused_computation.70 | convolution fusion | flops 1073741824 | bytes 6815744 | tf_op jit(solution)/shard_map/dot_general | solution.py:79
  99.0 154.8 %all-reduce.2.cloned.1.call-done = f32[512,2048]{1,0:T(8,128)} async-done(((f32[512,2048]{1,0:T(8,128)}), f32[512,2048]{1,0:T(8,128)}) %all-reduce.2.cloned.1.call-update) | async-done | bytes 4194320 | tf_op jit(solution)/shard_map/psum | solution.py:80
  253.8 4.9 %fusion.54 = bf16[512,2048]{1,0:T(8,128)(2,1)} fusion(f32[512,2048]{1,0:T(8,128)} %all-reduce.2.cloned.1.call-done, bf16[512,2048]{1,0:T(8,128)(2,1)} %param.11), kind=kLoop, calls=%fused_computation.58 | loop fusion | flops 3145728 | bytes 8388608 | tf_op jit(solution)/shard_map/convert_element_type | solution.py:81
  (36 shorter events, 1.7 us)
Async XLA Ops:
  7.2 88.5 %copy-start = (bf16[512,2048]{1,0:T(8,128)(2,1)S(1)}, bf16[512,2048]{1,0:T(8,128)(2,1)}, u32[]{:S(2)}) copy-start(bf16[512,2048]{1,0:T(8,128)(2,1)} %param.18) | copy-start | bytes 6291460
  7.2 15.4 %copy-start.6 = (f32[2048]{0:T(1024)S(1)}, f32[2048]{0:T(1024)}, u32[]{:S(2)}) copy-start(f32[2048]{0:T(1024)} %param.14) | copy-start | bytes 24580
  7.2 246.6 %all-reduce.2.cloned.1.call-start = ((), (), s32[]{:S(2)}) async-start(), calls=%async_computation | async-start | bytes 8388608 | tf_op jit(solution)/shard_map/psum | solution.py:80
  7.2 15.4 %copy-start.1 = (bf16[512,2048]{1,0:T(8,128)(2,1)S(1)}, bf16[512,2048]{1,0:T(8,128)(2,1)}, u32[]{:S(2)}) copy-start(bf16[512,2048]{1,0:T(8,128)(2,1)} %param.11) | copy-start | bytes 6291460
  7.3 15.4 %copy-start.5 = (bf16[2048,512]{1,0:T(8,128)(2,1)S(1)}, bf16[2048,512]{1,0:T(8,128)(2,1)}, u32[]{:S(2)}) copy-start(bf16[2048,512]{1,0:T(8,128)(2,1)} %param.15) | copy-start | bytes 6291460
  13.9 10.2 %copy-start.2 = (bf16[512,2,64]{0,2,1:T(8,128)(2,1)}, bf16[512,2,64]{0,2,1:T(8,128)(2,1)S(1)}, u32[]{:S(2)}) copy-start(bf16[512,2,64]{0,2,1:T(8,128)(2,1)S(1)} %pad_maximum_fusion.1) | copy-start | bytes 393220
  24.3 11.4 %copy-start.4 = (s32[512]{0:T(512)S(1)}, s32[512]{0:T(512)}, u32[]{:S(2)}) copy-start(s32[512]{0:T(512)} %param.12) | copy-start | bytes 6148
  28.3 12.7 %copy-start.3 = (bf16[512,128]{0,1:T(8,128)(2,1)}, bf16[512,128]{0,1:T(8,128)(2,1)S(1)}, u32[]{:S(2)}) copy-start(bf16[512,128]{0,1:T(8,128)(2,1)S(1)} %convolution_convert_fusion.1) | copy-start | bytes 393220
Sparse Core Ops, SparseCore 0:
  99.1 154.6 all-reduce.1
where the time goes:
time: 266 us
  waiting for transfers between devices  155 us (58%)
  matrix products  61.8 us (23%)
  blocking collectives  21.3 us (8%)
  between operations  14.2 us (5%)
  other arithmetic  10.6 us (4%)
    psum x1, waiting for transfers between devices, local_step(): full_sum = lax.psum(part_sum, 'tp')  155 us
    sub x4, matrix products, attend(): attn_probs = jax.nn.softmax(scores, axis=-1).astype(jnp.bfloat16)  30 us
    dot_general x4, matrix products, attend(): jnp.einsum('ngqk,knd->qngd', attn_probs, val_rows, preferred_element_type...  22 us
    all_gather x1, blocking collectives, local_step(): k_all = lax.all_gather(k_rot, 'cp', tiled=True)  8.71 us
    all_gather x1, blocking collectives, local_step(): v_all = lax.all_gather(v_new, 'cp', tiled=True)  7.28 us
    all_gather x1, blocking collectives, local_step(): doc_all = lax.all_gather(doc_id, 'cp', tiled=True)  5.34 us
  transfers between devices with their start and end apart: 1, of which 1 were waited for; matrix products, arithmetic and copies ran while one was open for 0% of the time, Pallas kernels for 0%

commit v1 on v0

v1 whole, which is shorter than its diff:
```python
import functools

import jax
import jax.numpy as jnp
from jax import lax
from jax.experimental import pallas as pl
from jax.experimental.pallas import tpu as pltpu
from jax.sharding import PartitionSpec as P

MESH = pl.DeviceIdType.MESH
F32 = jnp.float32
BF16 = jnp.bfloat16
ROWS = 512
BLK = 128
PIECE = 256
DM = 2048
TP = 4
SUB = 4
NEG = -1e30


def rcopy(src, dst, ssem, rsem, dev):
    return pltpu.make_async_remote_copy(src_ref=src, dst_ref=dst, send_sem=ssem, recv_sem=rsem, device_id=dev, device_id_type=MESH)


def places():
    dp, tp, cp = lax.axis_index('dp'), lax.axis_index('tp'), lax.axis_index('cp')
    y, c = cp // 2, cp % 2
    return dp, tp, cp, y, c


def rotate(t, cos_t, sin_t, low):
    turned = jnp.where(low, pltpu.roll(t, 96, 1), pltpu.roll(t, 32, 1))
    return t * cos_t + turned * sin_t


def front_kernel(x_ref, pos_ref, gain_ref, freq_ref, wq_ref, wk_ref, wv_ref, wo_ref,
                 q_ref, k_ref, v_ref, kv_out, wol_ref,
                 xv, wqv, wkv, h, cosv, sinv, kv_all, lsem, osem,
                 kv_ss, kv_rs, wz_ss, wz_rs):
    dp, tp, cp, y, c = places()
    lane_row = (dp * 4 + cp) * 64
    partner = (dp, tp, 2 * y + 1 - c)
    ynb = (dp, tp, 2 * (1 - y) + c)
    right, left = (dp, tp + 1, cp), (dp, tp - 1, cp)

    loads = []
    for b in range(4):
        loads.append(pltpu.make_async_copy(x_ref.at[pl.ds(b * BLK, BLK)], xv.at[pl.ds(b * BLK, BLK)], lsem.at[b]))
    loads.append(pltpu.make_async_copy(wk_ref, wkv.at[:, pl.ds(0, 128)], lsem.at[4]))
    loads.append(pltpu.make_async_copy(wv_ref, wkv.at[:, pl.ds(128, 128)], lsem.at[5]))
    loads.append(pltpu.make_async_copy(wq_ref, wqv, lsem.at[6]))
    for cpy in loads:
        cpy.start()

    barrier = pltpu.get_barrier_semaphore()
    for dev in (partner, ynb):
        pl.semaphore_signal(barrier, inc=1, device_id=dev, device_id_type=MESH)

    @pl.when(tp < TP - 1)
    def _():
        pl.semaphore_signal(barrier, inc=1, device_id=right, device_id_type=MESH)

    @pl.when(tp > 0)
    def _():
        pl.semaphore_signal(barrier, inc=1, device_id=left, device_id_type=MESH)

    lane = lax.broadcasted_iota(jnp.int32, (BLK, 128), 1)
    low = (lane % 64) < 32
    pos_t = pos_ref[...].T
    for b in range(4):
        ang = pos_t[:, b:b + 1] * freq_ref[...]
        rows = pl.ds(b * BLK, BLK)
        cosv[rows, :] = jnp.cos(ang)
        s = jnp.sin(ang)
        sinv[rows, :] = jnp.where(low, -s, s)

    pl.semaphore_wait(barrier, 3 + tp * (3 - tp) // 2)

    def wz(direction, src, half, own):
        part = pl.ds(half * 32, 32)
        src_ref = wo_ref.at[pl.ds(lane_row + half * 32, 32)] if own else wol_ref.at[src, part]
        return rcopy(src_ref, wol_ref.at[src, part], wz_ss.at[direction, src, half], wz_rs.at[src, half], right if direction == 0 else left)

    @pl.when(tp < TP - 1)
    def _():
        for half in range(2):
            wz(0, tp, half, True).start()

    @pl.when(tp > 0)
    def _():
        for half in range(2):
            wz(1, tp, half, True).start()

    def wz_step(s, half):
        @pl.when(tp >= s)
        def _():
            wz(0, tp - s, half, False).wait_recv()

        @pl.when((tp >= s) & (tp < TP - 1))
        def _():
            wz(0, tp - s, half, False).start()

        @pl.when(tp + s < TP)
        def _():
            wz(1, tp + s, half, False).wait_recv()

        @pl.when((tp + s < TP) & (tp > 0))
        def _():
            wz(1, tp + s, half, False).start()

    for b in range(4):
        rows = pl.ds(b * BLK, BLK)
        loads[b].wait()
        xf = xv[rows, :].astype(F32)
        inv = lax.rsqrt(jnp.mean(xf * xf, axis=-1, keepdims=True) + 1e-5)
        h[rows, :] = (xf * inv * gain_ref[...]).astype(BF16)

    loads[4].wait()
    loads[5].wait()
    my_a, my_b = cp * PIECE, (7 - cp) * PIECE
    nb_cp = 2 * (1 - y) + c
    nb = (nb_cp * PIECE, (7 - nb_cp) * PIECE)
    pt_cp = 2 * y + 1 - c
    pt = (pt_cp * PIECE, (7 - pt_cp) * PIECE)
    pd_cp = 2 * (1 - y) + 1 - c
    pd = (pd_cp * PIECE, (7 - pd_cp) * PIECE)
    mine = (my_a, my_b)

    def kvc(kind, half, row, dev):
        piece = kv_all.at[pl.ds(row, PIECE)]
        return rcopy(piece, piece, kv_ss.at[kind, half], kv_rs.at[kind, half], dev)

    for half in range(2):
        for bb in range(2):
            b = half * 2 + bb
            rows = pl.ds(b * BLK, BLK)
            kv = jnp.dot(h[rows, :], wkv[...], preferred_element_type=F32).astype(BF16)
            kf = kv[:, 0:128].astype(F32)
            k_rot = rotate(kf, cosv[rows, :], sinv[rows, :], low).astype(BF16)
            k_ref[:, rows] = k_rot.astype(F32).T.astype(BF16)
            v_ref[:, rows] = kv[:, 128:256].astype(F32).T.astype(BF16)
            dst = pl.ds(mine[half] + bb * BLK, BLK)
            kv_all[dst, 0:128] = k_rot
            kv_all[dst, 128:256] = kv[:, 128:256]
        kvc(0, half, mine[half], ynb).start()
        kvc(1, half, mine[half], partner).start()

    loads[6].wait()

    def q_rows(b):
        rows = pl.ds(b * BLK, BLK)
        qf = jnp.dot(h[rows, :], wqv[...], preferred_element_type=F32).astype(BF16).astype(F32)
        for g in range(4):
            cols = pl.ds(g * 128, 128)
            q_ref[rows, cols] = rotate(qf[:, g * 128:(g + 1) * 128], cosv[rows, :], sinv[rows, :], low).astype(BF16)

    q_rows(0)
    q_rows(1)
    wz_step(1, 0)
    q_rows(2)
    q_rows(3)
    wz_step(1, 1)
    wz_step(2, 0)
    for half in range(2):
        kvc(0, half, nb[half], ynb).wait_recv()
        kvc(2, half, nb[half], partner).start()
    wz_step(2, 1)
    for half in range(2):
        kvc(1, half, pt[half], partner).wait_recv()
        kvc(2, half, pd[half], partner).wait_recv()
    out = pltpu.make_async_copy(kv_all, kv_out, osem.at[0])
    out.start()
    wz_step(3, 0)
    wz_step(3, 1)
    for half in range(2):
        kvc(0, half, mine[half], ynb).wait_send()
        kvc(1, half, mine[half], partner).wait_send()
        kvc(2, half, nb[half], partner).wait_send()
    for s in range(0, TP):
        for half in range(2):
            @pl.when((tp >= s) & (tp < TP - 1))
            def _():
                wz(0, tp - s, half, s == 0).wait_send()

            @pl.when((tp + s < TP) & (tp > 0))
            def _():
                wz(1, tp + s, half, s == 0).wait_send()
    out.wait()


def front(x, pos8, gain, freq, wq, wk, wv, wo):
    any_, vm = pl.BlockSpec(memory_space=pl.ANY), pl.BlockSpec(memory_space=pltpu.VMEM)
    sds = jax.ShapeDtypeStruct
    dma = pltpu.SemaphoreType.DMA
    return pl.pallas_call(
        front_kernel,
        out_shape=(sds((ROWS, 512), BF16), sds((128, ROWS), BF16), sds((128, ROWS), BF16), sds((2048, 256), BF16), sds((TP, 64, DM), BF16)),
        in_specs=[any_, vm, vm, vm, any_, any_, any_, any_],
        out_specs=(vm, vm, vm, any_, any_),
        scratch_shapes=[
            pltpu.VMEM((ROWS, DM), BF16), pltpu.VMEM((DM, 512), BF16), pltpu.VMEM((DM, 256), BF16), pltpu.VMEM((ROWS, DM), BF16),
            pltpu.VMEM((ROWS, 128), F32), pltpu.VMEM((ROWS, 128), F32), pltpu.VMEM((2048, 256), BF16),
            dma((7,)), dma((1,)), dma((3, 2)), dma((3, 2)), dma((2, TP, 2)), dma((TP, 2)),
        ],
        compiler_params=pltpu.CompilerParams(collective_id=0, has_side_effects=True, vmem_limit_bytes=60 * 1024 * 1024),
        name='front',
    )(x, pos8, gain, freq, wq, wk, wv, wo)


def attend_kernel(first_ref, q_ref, kv_ref, pos_ref, o_ref, s_e, s_o):
    cp = lax.axis_index('cp')
    pos_t = pos_ref[...].T.astype(jnp.int32)
    low = lax.broadcasted_iota(jnp.int32, (1, 128), 1) < 64

    def halves(mat, n):
        zero = jnp.zeros_like(mat)
        other = pltpu.roll(mat.astype(F32), 64, 1).astype(BF16)
        if n == 0:
            return jnp.where(low, mat, zero), jnp.where(low, zero, other)
        return jnp.where(low, other, zero), jnp.where(low, zero, mat)

    def dot_t(a, b):
        return lax.dot_general(a, b, (((1,), (1,)), ((), ())), preferred_element_type=F32)

    def bias_of(base, width, t, p):
        u = base + lax.broadcasted_iota(jnp.int32, (BLK, width), 1)
        one = jnp.where((u <= t) & (u >= t - p), 0.0, NEG)
        return jnp.concatenate([one, one], axis=0)

    for b in range(4):
        piece = cp if b < 2 else 7 - cp
        t0 = piece * PIECE + (b % 2) * BLK
        p = pos_t[:, b:b + 1]
        t = t0 + lax.broadcasted_iota(jnp.int32, (BLK, 1), 0)
        first = t0 - first_ref[b]
        diag = t0 // BLK
        lo = first // BLK
        rows = pl.ds(b * BLK, BLK)

        def q_pairs(n):
            return jnp.concatenate([q_ref[rows, pl.ds(n * 256, 128)], q_ref[rows, pl.ds(n * 256 + 128, 128)]], axis=0)

        def put(n, out):
            o_ref[rows, pl.ds(n * 256, 128)] = out[0:BLK].astype(BF16)
            o_ref[rows, pl.ds(n * 256 + 128, 128)] = out[BLK:].astype(BF16)

        @pl.when(lo >= diag - 1)
        def _():
            base = jnp.maximum(diag - 1, 0) * BLK
            keys = pl.ds(pl.multiple_of(base, BLK), 2 * BLK)
            bias = bias_of(base, 2 * BLK, t, p)
            kk, vv = kv_ref[keys, 0:128], kv_ref[keys, 128:256]
            for n in range(2):
                qq = q_pairs(n)
                out = jnp.zeros((2 * BLK, 128), F32)
                for km, vm in zip(halves(kk, n), halves(vv, n)):
                    s = dot_t(qq, km) * 0.125 + bias
                    e = jnp.exp(s - jnp.max(s, axis=-1, keepdims=True))
                    pr = (e * (1.0 / jnp.sum(e, axis=-1, keepdims=True))).astype(BF16)
                    out = out + jnp.dot(pr, vm, preferred_element_type=F32)
                put(n, out)

        @pl.when(lo < diag - 1)
        def _():
            for n in range(2):
                qq = q_pairs(n)

                def score(kb, ms):
                    keys = pl.ds(pl.multiple_of(kb * BLK, BLK), BLK)
                    bias = bias_of(kb * BLK, BLK, t, p)
                    new = []
                    for km, s_ref, m in zip(halves(kv_ref[keys, 0:128], n), (s_e, s_o), ms):
                        s = dot_t(qq, km) * 0.125 + bias
                        s_ref[kb] = s
                        new.append(jnp.maximum(m, jnp.max(s, axis=-1, keepdims=True)))
                    return tuple(new)

                m0 = jnp.full((2 * BLK, 1), NEG, F32)
                ms = lax.fori_loop(lo, diag + 1, score, (m0, m0))

                def total(kb, ls):
                    return tuple(l + jnp.sum(jnp.exp(s_ref[kb] - m), axis=-1, keepdims=True) for l, s_ref, m in zip(ls, (s_e, s_o), ms))

                z0 = jnp.zeros((2 * BLK, 1), F32)
                ls = lax.fori_loop(lo, diag + 1, total, (z0, z0))
                rs = tuple(1.0 / l for l in ls)

                def mix(kb, out):
                    keys = pl.ds(pl.multiple_of(kb * BLK, BLK), BLK)
                    for vm, s_ref, m, r in zip(halves(kv_ref[keys, 128:256], n), (s_e, s_o), ms, rs):
                        pr = (jnp.exp(s_ref[kb] - m) * r).astype(BF16)
                        out = out + jnp.dot(pr, vm, preferred_element_type=F32)
                    return out

                put(n, lax.fori_loop(lo, diag + 1, mix, jnp.zeros((2 * BLK, 128), F32)))


def attend(first, q, kv, pos8):
    vm = pl.BlockSpec(memory_space=pltpu.VMEM)
    return pl.pallas_call(
        attend_kernel,
        out_shape=jax.ShapeDtypeStruct((ROWS, 512), BF16),
        in_specs=[pl.BlockSpec(memory_space=pltpu.SMEM), vm, vm, vm],
        out_specs=vm,
        scratch_shapes=[pltpu.VMEM((16, 2 * BLK, BLK), F32), pltpu.VMEM((16, 2 * BLK, BLK), F32)],
        compiler_params=pltpu.CompilerParams(vmem_limit_bytes=24 * 1024 * 1024),
        name='attend',
    )(first, q, kv, pos8)


def out_kernel(o_ref, x_ref, wo_ref, wol_ref, y_ref, o_all, wo_all, acc, xv, lsem, o_ss, o_rs, w_ss, f_ss, w_rs):
    dp, tp, cp, y, c = places()
    lane = dp * 4 + cp
    partner = (dp, tp, 2 * y + 1 - c)
    xnb = (1 - dp, tp, cp)
    ynb = (dp, tp, 2 * (1 - y) + c)
    dnb = (1 - dp, tp, 2 * (1 - y) + c)
    right, left = (dp, tp + 1, cp), (dp, tp - 1, cp)
    lanes = ((1 - dp) * 4 + cp, dp * 4 + 2 * (1 - y) + c, (1 - dp) * 4 + 2 * (1 - y) + c)
    peers = (xnb, ynb, dnb)
    p_lanes = tuple(l + 1 - 2 * c for l in (lane,) + lanes)

    mid, flip = tp * (3 - tp) // 2, tp // 2
    order = []
    for base in (1 + mid, 2 - 2 * mid, 3):
        order.append(base + flip * (3 - 2 * base))

    load_o = pltpu.make_async_copy(o_ref, o_all.at[tp], lsem.at[0])
    load_o.start()

    def slot(j, l):
        return wo_all.at[j, pl.ds(l * 64, 64)]

    load_l = [pltpu.make_async_copy(wol_ref.at[j], slot(j, lane), lsem.at[3 + i]) for i, j in enumerate(order)]
    for cpy in load_l:
        cpy.start()
    load_w = pltpu.make_async_copy(wo_ref, wo_all.at[tp], lsem.at[1])
    load_w.start()
    load_x = pltpu.make_async_copy(x_ref, xv, lsem.at[2])
    load_x.start()

    barrier = pltpu.get_barrier_semaphore()
    for dev in (partner,) + peers:
        pl.semaphore_signal(barrier, inc=1, device_id=dev, device_id_type=MESH)

    @pl.when(tp < TP - 1)
    def _():
        pl.semaphore_signal(barrier, inc=1, device_id=right, device_id_type=MESH)

    @pl.when(tp > 0)
    def _():
        pl.semaphore_signal(barrier, inc=1, device_id=left, device_id_type=MESH)

    pl.semaphore_wait(barrier, 5 + mid)

    def oc(direction, src, sub):
        part = o_all.at[src, pl.ds(sub * BLK, BLK)]
        return rcopy(part, part, o_ss.at[direction, src, sub], o_rs.at[src, sub], right if direction == 0 else left)

    load_o.wait()

    @pl.when(tp < TP - 1)
    def _():
        for sub in range(SUB):
            oc(0, tp, sub).start()

    @pl.when(tp > 0)
    def _():
        for sub in range(SUB):
            oc(1, tp, sub).start()

    def wsend(k, i, j, l, dev):
        return rcopy(slot(j, l), slot(j, l), w_ss.at[k, i], w_rs.at[j, l], dev)

    def wforward(k, i, j, l):
        return rcopy(slot(j, l), slot(j, l), f_ss.at[k, i], w_rs.at[j, l], partner)

    for k, j in enumerate(order):
        load_l[k].wait()
        for i, dev in enumerate(peers + (partner,)):
            wsend(k, i, j, lane, dev).start()

    def product(j, last):
        for n in range(4):
            cols = pl.ds(n * 512, 512)
            part = jnp.dot(o_all[j], wo_all[j, :, n * 512:(n + 1) * 512], preferred_element_type=F32)
            if last:
                y_ref[:, cols] = (acc[:, cols] + part).astype(BF16)
            else:
                acc[:, cols] += part

    load_w.wait()
    load_x.wait()
    for n in range(4):
        cols = pl.ds(n * 512, 512)
        acc[:, cols] = xv[:, cols].astype(F32)
    product(tp, False)

    def o_step(s, sub):
        @pl.when(tp >= s)
        def _():
            oc(0, tp - s, sub).wait_recv()

        @pl.when((tp >= s) & (tp < TP - 1))
        def _():
            oc(0, tp - s, sub).start()

        @pl.when(tp + s < TP)
        def _():
            oc(1, tp + s, sub).wait_recv()

        @pl.when((tp + s < TP) & (tp > 0))
        def _():
            oc(1, tp + s, sub).start()

    def w_step(k, i):
        j = order[k]
        wsend(k, i, j, lanes[i], peers[i]).wait_recv()
        wforward(k, i, j, lanes[i]).start()

    for k in range(3):
        s = k + 1
        o_step(s, 0)
        o_step(s, 1)
        w_step(k, 0)
        w_step(k, 1)
        o_step(s, 2)
        o_step(s, 3)
        w_step(k, 2)
        for l in p_lanes:
            wforward(k, 0, order[k], l).wait_recv()
        product(order[k], k == 2)

    for k, j in enumerate(order):
        for i, dev in enumerate(peers + (partner,)):
            wsend(k, i, j, lane, dev).wait_send()
        for i in range(3):
            wforward(k, i, j, lanes[i]).wait_send()
    for s in range(0, TP):
        for sub in range(SUB):
            @pl.when((tp >= s) & (tp < TP - 1))
            def _():
                oc(0, tp - s, sub).wait_send()

            @pl.when((tp + s < TP) & (tp > 0))
            def _():
                oc(1, tp + s, sub).wait_send()


def project_out(o, x, wo, wol):
    any_, vm = pl.BlockSpec(memory_space=pl.ANY), pl.BlockSpec(memory_space=pltpu.VMEM)
    dma = pltpu.SemaphoreType.DMA
    return pl.pallas_call(
        out_kernel,
        out_shape=jax.ShapeDtypeStruct((ROWS, DM), BF16),
        in_specs=[any_, any_, any_, any_],
        out_specs=vm,
        scratch_shapes=[
            pltpu.VMEM((TP, ROWS, 512), BF16), pltpu.VMEM((TP, 512, DM), BF16), pltpu.VMEM((ROWS, DM), F32), pltpu.VMEM((ROWS, DM), BF16),
            dma((6,)), dma((2, TP, SUB)), dma((TP, SUB)), dma((3, 4)), dma((3, 3)), dma((TP, 8)),
        ],
        compiler_params=pltpu.CompilerParams(collective_id=1, has_side_effects=True, vmem_limit_bytes=60 * 1024 * 1024),
        name='project_out',
    )(o, x, wo, wol)


def solution(mesh):
    def local_step(x, doc_id, pos, gain, wq, wk, wv, wo, inv_freq):
        pos8 = jnp.pad(pos.reshape(4, BLK).astype(F32), ((0, 4), (0, 0)))
        freq = jnp.tile(inv_freq.reshape(1, 32), (1, 4))
        first = pos.reshape(4, BLK)[:, 0]
        q, k, v, kv, wol = front(x, pos8, gain.reshape(1, DM), freq, wq, wk, wv, wo)
        o = attend(first, q, kv, pos8)
        y = project_out(o, x, wo, wol)
        return y, k.T.reshape(ROWS, 2, 64), v.T.reshape(ROWS, 2, 64)

    row_spec = P(('dp', 'cp'))
    in_specs = (P(('dp', 'cp'), None), row_spec, row_spec, P(), P(None, 'tp'), P(None, 'tp'), P(None, 'tp'), P('tp', None), P())
    out_specs = (P(('dp', 'cp'), None), P(('dp', 'cp'), 'tp', None), P(('dp', 'cp'), 'tp', None))
    return jax.shard_map(local_step, mesh=mesh, in_specs=in_specs, out_specs=out_specs, check_vma=False)
```

time: 266 us -> 83.5 us (0.31)
  waiting for transfers between devices: 155 us -> 0 us
  Pallas kernels: 0 us -> 70.5 us
  matrix products: 61.8 us -> 0 us
  blocking collectives: 21.3 us -> 0 us
  between operations: 14.2 us -> 0.7 us
  other arithmetic: 10.6 us -> 0.68 us
  local copies, waits for them, and re-layouts: 2.63 us -> 10.2 us
    psum x1 -> x0, waiting for transfers between devices: 155 us -> none  [local_step(): full_sum = lax.psum(part_sum, 'tp')]
    pallas_call x0 -> x3, Pallas kernels: none -> 70.5 us  [the longest x1 41.4 us: project_out(): pl.pallas_call(out_kernel, out_shape=jax.ShapeDtypeStruct((ROWS, DM), BF1...]
    dot_general x8 -> x0, matrix products: 31.9 us -> none  [the longest x4 22 us: attend(): jnp.einsum('ngqk,knd->qngd', attn_probs, val_rows, preferred_element_type...]
    sub x4 -> x0, matrix products: 30 us -> none  [attend(): attn_probs = jax.nn.softmax(scores, axis=-1).astype(jnp.bfloat16)]
    all_gather x3 -> x0, blocking collectives: 21.3 us -> none  [the longest x1 8.71 us: local_step(): k_all = lax.all_gather(k_rot, 'cp', tiled=True)]
    unnamed x15, local copies, waits for them, and re-layouts: 1.02 us -> 7.57 us
    convert_element_type x2 -> x1, other arithmetic: 5.66 us -> 0.68 us  [local_step(): pos8 = jnp.pad(pos.reshape(4, BLK).astype(F32), ((0, 4), (0, 0)))]
  transfers between devices with their start and end apart: 1 -> 0, of which waited for: 1 -> 0; matrix products, arithmetic and copies ran while one was open for 0% -> 0% of each run, Pallas kernels for 0% -> 0%
where the time goes in v1:
time: 83.5 us; the launch traced here: 82.1 us
  Pallas kernels  70.5 us (84%)
  local copies, waits for them, and re-layouts  10.2 us (12%)
    pallas_call x1, Pallas kernels, project_out(): pl.pallas_call(out_kernel, out_shape=jax.ShapeDtypeStruct((ROWS, DM), BF1...  41.4 us
    pallas_call x1, Pallas kernels, front(): pl.pallas_call(front_kernel, out_shape=(sds((ROWS, 512), BF16), sds((128,...  24 us
    unnamed x15, local copies, waits for them, and re-layouts  7.57 us
    pallas_call x1, Pallas kernels, attend(): pl.pallas_call(attend_kernel, out_shape=jax.ShapeDtypeStruct((ROWS, 512),...  5.12 us

profile of v1, /device:TPU:0, one launch (start us, length us, event | category | flops | bytes accessed | tf_op | source)
XLA Modules:
  0.0 82.1 jit_solution(2307738227939106548)
XLA Ops:
  0.6 0.8 slice_reduce_fusion.first_ref
  1.4 0.7 tile.8
  2.1 0.6 tile.9.freq_ref
  2.7 0.7 bitcast_convert_fusion
  3.4 0.6 pad.4.pos_ref
  4.0 0.0 copy-start.3
  4.0 24.0 %front.1 = (bf16[512,512]{1,0:T(8,128)(2,1)}, bf16[128,512]{1,0:T(8,128)(2,1)}, bf16[128,512]{1,0:T(8,128)(2,1)}, bf16[2048,256]{1,0:T(8,128)(2,1)}, bf16[4,64,2048]{2,1,0:T(8,128)(2,1)}) custom-call(bf16[512,2048]{1,0:T(8,128)(2,1)} %x_ref.3, f32[8,128]{1,0:T(8,128)} %pad.4.pos_ref, f32[1,2048]{1,0:T(1,128)} %bitcast.12, f32[1,128]{1,0:T(1,128)} %tile.9.freq_ref, ...), custom_call_target="tpu_custom_call" | custom-call | tf_op jit(solution)/shard_map/front/pallas_call | solution.py:196
  28.0 0.0 copy-done.3
  28.0 0.0 copy-start.1
  28.0 1.2 %copy-done.1 = bf16[2048,256]{1,0:T(8,128)(2,1)S(1)} copy-done((bf16[2048,256]{1,0:T(8,128)(2,1)S(1)}, bf16[2048,256]{1,0:T(8,128)(2,1)}, u32[]{:S(2)}) %copy-start.1) | copy-done | bytes 1048600
  29.2 0.0 copy-start.2
  29.2 1.0 %copy-done.2 = bf16[512,512]{1,0:T(8,128)(2,1)S(1)} copy-done((bf16[512,512]{1,0:T(8,128)(2,1)S(1)}, bf16[512,512]{1,0:T(8,128)(2,1)}, u32[]{:S(2)}) %copy-start.2) | copy-done | bytes 524312
  30.3 5.1 %attend.1.o_ref = bf16[512,512]{1,0:T(8,128)(2,1)S(1)} custom-call(s32[4]{0:T(128)S(1)} %slice_reduce_fusion.first_ref, bf16[512,512]{1,0:T(8,128)(2,1)S(1)} %copy-done.2, bf16[2048,256]{1,0:T(8,128)(2,1)S(1)} %copy-done.1, f32[8,128]{1,0:T(8,128)S(1)} %copy-done.3), custom_call_target="tpu_custom_call" | custom-call | tf_op jit(solution)/shard_map/attend/pallas_call | solution.py:301
  35.4 0.0 copy-start
  35.4 0.8 copy-done
  36.2 41.4 %project_out.1 = bf16[512,2048]{1,0:T(8,128)(2,1)} custom-call(bf16[512,512]{1,0:T(8,128)(2,1)} %copy-done, bf16[512,2048]{1,0:T(8,128)(2,1)} %x_ref.3, bf16[512,2048]{1,0:T(8,128)(2,1)} %wo_ref.3, bf16[4,64,2048]{2,1,0:T(8,128)(2,1)} %get-tuple-element.10.wol_ref), custom_call_target="tpu_custom_call" | custom-call | tf_op jit(solution)/shard_map/project_out/pallas_call | solution.py:454
  77.6 0.0 copy-start.5
  77.6 0.0 copy-start.4
  77.6 3.2 %copy.14 = bf16[512,2048]{1,0:T(8,128)(2,1)} copy(bf16[512,2048]{1,0:T(8,128)(2,1)} %project_out.1) | data formatting | bytes 4194304
  80.8 0.0 copy-done.5
  80.8 0.7 copy.15
  81.5 0.0 copy-done.4
  81.5 0.7 copy.16
Async XLA Ops:
  4.0 24.0 %copy-start.3 = (f32[8,128]{1,0:T(8,128)S(1)}, f32[8,128]{1,0:T(8,128)}, u32[]{:S(2)}) copy-start(f32[8,128]{1,0:T(8,128)} %pad.4.pos_ref) | copy-start | bytes 12292
  28.0 1.2 %copy-start.1 = (bf16[2048,256]{1,0:T(8,128)(2,1)S(1)}, bf16[2048,256]{1,0:T(8,128)(2,1)}, u32[]{:S(2)}) copy-start(bf16[2048,256]{1,0:T(8,128)(2,1)} %get-tuple-element.9.kv_ref) | copy-start | bytes 3145732
  29.2 1.0 %copy-start.2 = (bf16[512,512]{1,0:T(8,128)(2,1)S(1)}, bf16[512,512]{1,0:T(8,128)(2,1)}, u32[]{:S(2)}) copy-start(bf16[512,512]{1,0:T(8,128)(2,1)} %get-tuple-element.8.q_ref) | copy-start | bytes 1572868
  35.4 0.8 copy-start
  77.6 3.2 %copy-start.5 = (bf16[128,512]{1,0:T(8,128)(2,1)S(1)}, bf16[128,512]{1,0:T(8,128)(2,1)}, u32[]{:S(2)}) copy-start(bf16[128,512]{1,0:T(8,128)(2,1)} %get-tuple-element.11) | copy-start | bytes 393220
  77.6 3.9 %copy-start.4 = (bf16[128,512]{1,0:T(8,128)(2,1)S(1)}, bf16[128,512]{1,0:T(8,128)(2,1)}, u32[]{:S(2)}) copy-start(bf16[128,512]{1,0:T(8,128)(2,1)} %get-tuple-element.12) | copy-start | bytes 393220

commit v2 on v0

v2 whole, which is shorter than its diff:
```python
import jax
import jax.numpy as jnp
from jax import lax
from jax.experimental import pallas as pl
from jax.experimental.pallas import tpu as pltpu
from jax.sharding import PartitionSpec as P

MESH = pl.DeviceIdType.MESH
F32 = jnp.float32
BF16 = jnp.bfloat16
ROWS = 512
BLK = 128
PIECE = 256
DM = 2048
TP = 4
NEG = -1e30


def rcopy(src, dst, ssem, rsem, dev):
    return pltpu.make_async_remote_copy(src_ref=src, dst_ref=dst, send_sem=ssem, recv_sem=rsem, device_id=dev, device_id_type=MESH)


def layer_kernel(x_ref, pos_ref, gain_ref, freq_ref, wq_ref, wk_ref, wv_ref, wo_ref,
                 y_ref, kt_ref, vt_ref,
                 xv, wqv, wkv, h, cosv, sinv, kv_all, kk, vv, qm, st, m_s, l_s, a_s, o_all, wo_all, acc,
                 lsem, kv_ss, kv_rs, wz_ss, w_ss, f_ss, w_rs, o_ss, o_rs):
    dp, tp, cp = lax.axis_index('dp'), lax.axis_index('tp'), lax.axis_index('cp')
    y, c = cp // 2, cp % 2
    lane = dp * 4 + cp
    partner = (dp, tp, 2 * y + 1 - c)
    xnb = (1 - dp, tp, cp)
    ynb = (dp, tp, 2 * (1 - y) + c)
    dnb = (1 - dp, tp, 2 * (1 - y) + c)
    right, left = (dp, tp + 1, cp), (dp, tp - 1, cp)
    lanes = ((1 - dp) * 4 + cp, dp * 4 + 2 * (1 - y) + c, (1 - dp) * 4 + 2 * (1 - y) + c)
    peers = (xnb, ynb, dnb)
    p_lanes = tuple(l + 1 - 2 * c for l in (lane,) + lanes)
    mid, flip = tp * (3 - tp) // 2, tp // 2
    order = []
    for base in (1 + mid, 2 - 2 * mid, 3):
        order.append(base + flip * (3 - 2 * base))

    barrier = pltpu.get_barrier_semaphore()
    for dev in (partner,) + peers + tuple((dp, j, cp) for j in order):
        pl.semaphore_signal(barrier, inc=1, device_id=dev, device_id_type=MESH)

    loads = []
    for b in range(2):
        rows = pl.ds(b * PIECE, PIECE)
        loads.append(pltpu.make_async_copy(x_ref.at[rows], xv.at[rows], lsem.at[b]))
    loads.append(pltpu.make_async_copy(wk_ref, wkv.at[:, pl.ds(0, 128)], lsem.at[2]))
    loads.append(pltpu.make_async_copy(wv_ref, wkv.at[:, pl.ds(128, 128)], lsem.at[3]))
    loads.append(pltpu.make_async_copy(wq_ref, wqv, lsem.at[4]))
    loads.append(pltpu.make_async_copy(wo_ref, wo_all.at[tp], lsem.at[5]))
    for cpy in loads:
        cpy.start()

    lane_i = lax.broadcasted_iota(jnp.int32, (BLK, 128), 1)
    pos_t = jnp.concatenate([pos_ref[...].astype(F32), jnp.zeros((4, BLK), F32)], axis=0).T
    freq = jnp.concatenate([freq_ref[...]] * 4, axis=1)
    pos_l = jnp.zeros((BLK, 128), F32)
    for b in range(4):
        pos_l = jnp.where(lane_i // 32 == b, pos_t[:, b:b + 1], pos_l)
    ang = pos_l * freq
    tables = (jnp.cos(ang), jnp.sin(ang))
    low32 = (lane_i % 64) < 32
    for b in range(4):
        for ref, tab in zip((cosv, sinv), tables):
            t = jnp.where(lane_i // 32 == b, tab, 0.0)
            t = t + pltpu.roll(t, 32, 1)
            t = t + pltpu.roll(t, 64, 1)
            if ref is sinv:
                t = jnp.where(low32, -t, t)
            ref[b * BLK:(b + 1) * BLK, :] = t

    pl.semaphore_wait(barrier, 7)

    def slot(j, l):
        return wo_all.at[j, pl.ds(l * 64, 64)]

    for k, j in enumerate(order):
        rcopy(wo_ref.at[pl.ds(lane * 64, 64)], slot(tp, lane), wz_ss.at[k], w_rs.at[tp, lane], (dp, j, cp)).start()

    def wz(k):
        return rcopy(slot(order[k], lane), slot(order[k], lane), wz_ss.at[k], w_rs.at[order[k], lane], (dp, order[k], cp))

    def wsend(k, i, l, dev):
        return rcopy(slot(order[k], l), slot(order[k], l), w_ss.at[k, i], w_rs.at[order[k], l], dev)

    def wforward(k, i, l):
        return rcopy(slot(order[k], l), slot(order[k], l), f_ss.at[k, i], w_rs.at[order[k], l], partner)

    def w_arrive(k):
        wz(k).wait_recv()
        for i, dev in enumerate(peers + (partner,)):
            wsend(k, i, lane, dev).start()

    def w_step(k, i):
        wsend(k, i, lanes[i], peers[i]).wait_recv()
        wforward(k, i, lanes[i]).start()

    def norm(b):
        rows = pl.ds(b * PIECE, PIECE)
        xf = xv[rows, :].astype(F32)
        inv = lax.rsqrt(jnp.mean(xf * xf, axis=-1, keepdims=True) + 1e-5)
        h[rows, :] = (xf * inv * gain_ref[...]).astype(BF16)

    low = lax.broadcasted_iota(jnp.int32, (PIECE, 128), 1)
    low_head = low < 64
    low_half = (low % 64) < 32

    def rotate(t, rows):
        turned = jnp.where(low_half, pltpu.roll(t, 96, 1), pltpu.roll(t, 32, 1))
        return t * cosv[rows, :] + turned * sinv[rows, :]

    mine = (cp, 7 - cp)
    nb_cp, pt_cp, pd_cp = 2 * (1 - y) + c, 2 * y + 1 - c, 2 * (1 - y) + 1 - c
    nb, pt, pd = (nb_cp, 7 - nb_cp), (pt_cp, 7 - pt_cp), (pd_cp, 7 - pd_cp)

    def kvc(kind, half, piece, dev):
        return rcopy(kv_all.at[piece], kv_all.at[piece], kv_ss.at[kind, half], kv_rs.at[kind, half], dev)

    for b in range(2):
        rows = slice(b * PIECE, (b + 1) * PIECE)
        loads[b].wait()
        norm(b)
        if b == 0:
            loads[2].wait()
            loads[3].wait()
        kv = jnp.dot(h[rows, :], wkv[...], preferred_element_type=F32).astype(BF16)
        k_rot = rotate(kv[:, 0:128].astype(F32), rows).astype(BF16)
        kv_all[mine[b], :, 0:128] = k_rot
        kv_all[mine[b], :, 128:256] = kv[:, 128:256]
        kt_ref[:, rows] = k_rot.astype(F32).T.astype(BF16)
        vt_ref[:, rows] = kv[:, 128:256].astype(F32).T.astype(BF16)
        kvc(0, b, mine[b], ynb).start()
        kvc(1, b, mine[b], partner).start()

    loads[4].wait()
    for b in range(2):
        rows = slice(b * PIECE, (b + 1) * PIECE)
        qf = jnp.dot(h[rows, :], wqv[...], preferred_element_type=F32).astype(BF16).astype(F32)
        for g in range(4):
            q = rotate(qf[:, g * 128:(g + 1) * 128], rows).astype(BF16)
            q = (q.astype(F32) * 0.125).astype(BF16)
            zero = jnp.zeros_like(q)
            at = (g % 2) * 2 * PIECE
            qm[g // 2, b, at:at + PIECE, :] = jnp.where(low_head, q, zero)
            qm[g // 2, b, at + PIECE:at + 2 * PIECE, :] = jnp.where(low_head, zero, q)

    w_arrive(0)
    for b in range(2):
        kvc(0, b, nb[b], ynb).wait_recv()
        kvc(2, b, nb[b], partner).start()
    for b in range(2):
        kvc(1, b, pt[b], partner).wait_recv()
        kvc(2, b, pd[b], partner).wait_recv()

    def double(piece, carry):
        for i, ref in enumerate((kk, vv)):
            t = kv_all[piece, :, i * 128:(i + 1) * 128]
            r = pltpu.roll(t.astype(F32), 64, 1).astype(BF16)
            ref[0, piece] = jnp.where(low_head, t, r)
            ref[1, piece] = jnp.where(low_head, r, t)
        return carry

    lax.fori_loop(0, 8, double, 0)

    q_iota = lax.broadcasted_iota(jnp.int32, (PIECE, PIECE), 0)
    k_iota = lax.broadcasted_iota(jnp.int32, (PIECE, PIECE), 1)

    def attend(n, b):
        piece = mine[b]
        pos_c = jnp.concatenate([pos_t[:, 2 * b:2 * b + 1], pos_t[:, 2 * b + 1:2 * b + 2]], axis=0).astype(jnp.int32)
        start_c = q_iota[:, 0:1] - pos_c
        m_s[...] = jnp.full(m_s.shape, NEG, F32)
        l_s[...] = jnp.zeros(l_s.shape, F32)
        a_s[...] = jnp.zeros(a_s.shape, F32)

        def score(kp, carry):
            u = k_iota + (kp - piece) * PIECE
            bias = jnp.where((u <= q_iota) & (u >= start_c), 0.0, NEG)
            for g in range(4):
                r = slice(g * PIECE, (g + 1) * PIECE)
                s = lax.dot_general(qm[n, b, r, :], kk[n, kp], (((1,), (1,)), ((), ())), preferred_element_type=F32) + bias
                st[kp, r, :] = s
                m_s[r, :] = jnp.maximum(m_s[r, :], jnp.maximum(s[:, 0:128], s[:, 128:256]))
            return carry

        lax.fori_loop(0, piece + 1, score, 0)
        m_s[...] = jnp.broadcast_to(jnp.max(m_s[...], axis=-1, keepdims=True), m_s.shape)

        def expo(kp, carry):
            for g in range(4):
                r = slice(g * PIECE, (g + 1) * PIECE)
                e0 = jnp.exp(st[kp, r, 0:128] - m_s[r, :])
                e1 = jnp.exp(st[kp, r, 128:256] - m_s[r, :])
                st[kp, r, 0:128] = e0
                st[kp, r, 128:256] = e1
                l_s[r, :] += e0 + e1
            return carry

        lax.fori_loop(0, piece + 1, expo, 0)
        l_s[...] = jnp.broadcast_to(1.0 / jnp.sum(l_s[...], axis=-1, keepdims=True), l_s.shape)

        def mix(kp, carry):
            for g in range(4):
                r = slice(g * PIECE, (g + 1) * PIECE)
                p = jnp.concatenate([st[kp, r, 0:128] * l_s[r, :], st[kp, r, 128:256] * l_s[r, :]], axis=1).astype(BF16)
                a_s[r, :] += jnp.dot(p, vv[n, kp], preferred_element_type=F32)
            return carry

        lax.fori_loop(0, piece + 1, mix, 0)
        for a in range(2):
            even = a_s[2 * a * PIECE:(2 * a + 1) * PIECE, :]
            odd = a_s[(2 * a + 1) * PIECE:(2 * a + 2) * PIECE, :]
            o_all[tp, n, b * PIECE:(b + 1) * PIECE, a * 128:(a + 1) * 128] = jnp.where(low_head, even, odd).astype(BF16)

    def oc(direction, src, sub):
        part = o_all.at[src, sub // 2, pl.ds((sub % 2) * PIECE, PIECE)]
        return rcopy(part, part, o_ss.at[direction, src, sub], o_rs.at[src, sub], right if direction == 0 else left)

    for n in range(2):
        for b in range(2):
            attend(n, b)
            sub = 2 * n + b

            @pl.when(tp < TP - 1)
            def _():
                oc(0, tp, sub).start()

            @pl.when(tp > 0)
            def _():
                oc(1, tp, sub).start()

            if sub < 2:
                w_arrive(sub + 1)

    def product(j, rows, last):
        for t in range(4):
            cols = slice(t * 512, (t + 1) * 512)
            part = jnp.dot(o_all[j, 0, rows, :], wo_all[j, 0:256, cols], preferred_element_type=F32)
            part += jnp.dot(o_all[j, 1, rows, :], wo_all[j, 256:512, cols], preferred_element_type=F32)
            if last:
                y_ref[rows, cols] = (acc[rows, cols] + part).astype(BF16)
            else:
                acc[rows, cols] += part

    every = slice(0, ROWS)
    loads[5].wait()
    for t in range(4):
        cols = slice(t * 512, (t + 1) * 512)
        acc[:, cols] = xv[:, cols].astype(F32)
    product(tp, every, False)

    def o_step(s, sub):
        @pl.when(tp >= s)
        def _():
            oc(0, tp - s, sub).wait_recv()

        @pl.when((tp >= s) & (tp < TP - 1))
        def _():
            oc(0, tp - s, sub).start()

        @pl.when(tp + s < TP)
        def _():
            oc(1, tp + s, sub).wait_recv()

        @pl.when((tp + s < TP) & (tp > 0))
        def _():
            oc(1, tp + s, sub).start()

    for k in range(3):
        s = k + 1
        o_step(s, 0)
        w_step(k, 0)
        o_step(s, 1)
        w_step(k, 1)
        o_step(s, 2)
        w_step(k, 2)
        o_step(s, 3)
        for l in p_lanes:
            wforward(k, 0, l).wait_recv()
        product(order[k], every, k == 2)

    for b in range(2):
        kvc(0, b, mine[b], ynb).wait_send()
        kvc(1, b, mine[b], partner).wait_send()
        kvc(2, b, nb[b], partner).wait_send()
    for k in range(3):
        wz(k).wait_send()
        for i, dev in enumerate(peers + (partner,)):
            wsend(k, i, lane, dev).wait_send()
        for i in range(3):
            wforward(k, i, lanes[i]).wait_send()
    for s in range(0, TP):
        for sub in range(4):
            @pl.when((tp >= s) & (tp < TP - 1))
            def _():
                oc(0, tp - s, sub).wait_send()

            @pl.when((tp + s < TP) & (tp > 0))
            def _():
                oc(1, tp + s, sub).wait_send()


def layer(x, pos, gain, freq, wq, wk, wv, wo):
    hbm, vm = pl.BlockSpec(memory_space=pltpu.HBM), pl.BlockSpec(memory_space=pltpu.VMEM)
    sds = jax.ShapeDtypeStruct
    dma = pltpu.SemaphoreType.DMA
    return pl.pallas_call(
        layer_kernel,
        out_shape=(sds((ROWS, DM), BF16), sds((128, ROWS), BF16), sds((128, ROWS), BF16)),
        in_specs=[hbm, vm, vm, vm, hbm, hbm, hbm, hbm],
        out_specs=(vm, vm, vm),
        scratch_shapes=[
            pltpu.VMEM((ROWS, DM), BF16), pltpu.VMEM((DM, 512), BF16), pltpu.VMEM((DM, 256), BF16), pltpu.VMEM((ROWS, DM), BF16),
            pltpu.VMEM((ROWS, 128), F32), pltpu.VMEM((ROWS, 128), F32), pltpu.VMEM((8, PIECE, 256), BF16),
            pltpu.VMEM((2, 8, PIECE, 128), BF16), pltpu.VMEM((2, 8, PIECE, 128), BF16), pltpu.VMEM((2, 2, 4 * PIECE, 128), BF16),
            pltpu.VMEM((8, 4 * PIECE, PIECE), F32),
            pltpu.VMEM((4 * PIECE, 128), F32), pltpu.VMEM((4 * PIECE, 128), F32), pltpu.VMEM((4 * PIECE, 128), F32),
            pltpu.VMEM((TP, 2, ROWS, 256), BF16), pltpu.VMEM((TP, 512, DM), BF16), pltpu.VMEM((ROWS, DM), F32),
            dma((6,)), dma((3, 2)), dma((3, 2)), dma((3,)), dma((3, 4)), dma((3, 3)), dma((TP, 8)), dma((2, TP, 4)), dma((TP, 4)),
        ],
        compiler_params=pltpu.CompilerParams(collective_id=0, has_side_effects=True, vmem_limit_bytes=60 * 1024 * 1024),
        name='layer',
    )(x, pos, gain, freq, wq, wk, wv, wo)


def solution(mesh):
    def local_step(x, doc_id, pos, gain, wq, wk, wv, wo, inv_freq):
        y, kt, vt = layer(x, pos.reshape(4, BLK), gain.reshape(1, DM), inv_freq.reshape(1, 32), wq, wk, wv, wo)
        return y, kt.T.reshape(ROWS, 2, 64), vt.T.reshape(ROWS, 2, 64)

    row_spec = P(('dp', 'cp'))
    in_specs = (P(('dp', 'cp'), None), row_spec, row_spec, P(), P(None, 'tp'), P(None, 'tp'), P(None, 'tp'), P('tp', None), P())
    out_specs = (P(('dp', 'cp'), None), P(('dp', 'cp'), 'tp', None), P(('dp', 'cp'), 'tp', None))
    return jax.shard_map(local_step, mesh=mesh, in_specs=in_specs, out_specs=out_specs, check_vma=False)
```

time: 266 us -> 77.7 us (0.29)
  waiting for transfers between devices: 155 us -> 0 us
  Pallas kernels: 0 us -> 72.3 us
  matrix products: 61.8 us -> 0 us
  blocking collectives: 21.3 us -> 0 us
  between operations: 14.2 us -> 0.66 us
  other arithmetic: 10.6 us -> 0 us
    psum x1 -> x0, waiting for transfers between devices: 155 us -> none  [local_step(): full_sum = lax.psum(part_sum, 'tp')]
    pallas_call x0 -> x1, Pallas kernels: none -> 72.3 us  [layer(): pl.pallas_call(layer_kernel, out_shape=(sds((ROWS, DM), BF16), sds((128,...]
    dot_general x8 -> x0, matrix products: 31.9 us -> none  [the longest x4 22 us: attend(): jnp.einsum('ngqk,knd->qngd', attn_probs, val_rows, preferred_element_type...]
    sub x4 -> x0, matrix products: 30 us -> none  [attend(): attn_probs = jax.nn.softmax(scores, axis=-1).astype(jnp.bfloat16)]
    all_gather x3 -> x0, blocking collectives: 21.3 us -> none  [the longest x1 8.71 us: local_step(): k_all = lax.all_gather(k_rot, 'cp', tiled=True)]
    convert_element_type x2 -> x0, other arithmetic: 5.66 us -> none  [the longest x1 4.9 us: local_step(): y_out = (x_in.astype(jnp.float32) + full_sum).astype(jnp.bfloat16)]
    unnamed x15 -> x7, local copies, waits for them, and re-layouts: 1.02 us -> 4.52 us
  transfers between devices with their start and end apart: 1 -> 0, of which waited for: 1 -> 0; matrix products, arithmetic and copies ran while one was open for 0% -> 0% of each run, Pallas kernels for 0% -> 0%
where the time goes in v2:
time: 77.7 us; the launch traced here: 77.5 us
  Pallas kernels  72.3 us (93%)
  local copies, waits for them, and re-layouts  4.52 us (6%)
    pallas_call x1, Pallas kernels, layer(): pl.pallas_call(layer_kernel, out_shape=(sds((ROWS, DM), BF16), sds((128,...  72.3 us
    unnamed x7, local copies, waits for them, and re-layouts  4.52 us

profile of v2, /device:TPU:0, one launch (start us, length us, event | category | flops | bytes accessed | tf_op | source)
XLA Modules:
  0.0 77.5 jit_solution(7314664135184082673)
XLA Ops:
  0.6 72.3 %layer.1 = (bf16[512,2048]{1,0:T(8,128)(2,1)}, bf16[128,512]{1,0:T(8,128)(2,1)}, bf16[128,512]{1,0:T(8,128)(2,1)}) custom-call(bf16[512,2048]{1,0:T(8,128)(2,1)} %x_ref.1, s32[4,128]{1,0:T(4,128)} %bitcast.12, f32[1,2048]{1,0:T(1,128)} %bitcast.11, f32[1,32]{1,0:T(1,128)} %bitcast.13, bf16[2048,512]{1,0:T(8,128)(2,1)} %wq_ref.1, bf16[2048,128]{1,0:T(8,128)(2,1)} %wk_ref.1, ...), custom_call_target="tpu_custom_call" | custom-call | tf_op jit(solution)/shard_map/layer/pallas_call | solution.py:311
  72.9 0.0 copy-start.1
  72.9 0.0 copy-start
  72.9 3.2 %copy.14 = bf16[512,2048]{1,0:T(8,128)(2,1)} copy(bf16[512,2048]{1,0:T(8,128)(2,1)} %get-tuple-element.12) | data formatting | bytes 4194304
  76.1 0.0 copy-done.1
  76.1 0.7 copy.15
  76.8 0.0 copy-done
  76.8 0.7 copy.16
Async XLA Ops:
  72.9 3.2 %copy-start.1 = (bf16[128,512]{1,0:T(8,128)(2,1)S(1)}, bf16[128,512]{1,0:T(8,128)(2,1)}, u32[]{:S(2)}) copy-start(bf16[128,512]{1,0:T(8,128)(2,1)} %get-tuple-element.7) | copy-start | bytes 393220
  72.9 3.9 %copy-start = (bf16[128,512]{1,0:T(8,128)(2,1)S(1)}, bf16[128,512]{1,0:T(8,128)(2,1)}, u32[]{:S(2)}) copy-start(bf16[128,512]{1,0:T(8,128)(2,1)} %get-tuple-element.8) | copy-start | bytes 393220

commit v3 on v2

--- a/solution.py
+++ b/solution.py
@@ -41,8 +41,16 @@
         order.append(base + flip * (3 - 2 * base))
 
     barrier = pltpu.get_barrier_semaphore()
-    for dev in (partner,) + peers + tuple((dp, j, cp) for j in order):
+    for dev in (partner,) + peers:
         pl.semaphore_signal(barrier, inc=1, device_id=dev, device_id_type=MESH)
+
+    @pl.when(tp < TP - 1)
+    def _():
+        pl.semaphore_signal(barrier, inc=1, device_id=right, device_id_type=MESH)
+
+    @pl.when(tp > 0)
+    def _():
+        pl.semaphore_signal(barrier, inc=1, device_id=left, device_id_type=MESH)
 
     loads = []
     for b in range(2):
@@ -52,8 +60,8 @@
     loads.append(pltpu.make_async_copy(wv_ref, wkv.at[:, pl.ds(128, 128)], lsem.at[3]))
     loads.append(pltpu.make_async_copy(wq_ref, wqv, lsem.at[4]))
     loads.append(pltpu.make_async_copy(wo_ref, wo_all.at[tp], lsem.at[5]))
-    for cpy in loads:
-        cpy.start()
+    for i in (5, 0, 2, 3, 1, 4):
+        loads[i].start()
 
     lane_i = lax.broadcasted_iota(jnp.int32, (BLK, 128), 1)
     pos_t = jnp.concatenate([pos_ref[...].astype(F32), jnp.zeros((4, BLK), F32)], axis=0).T
@@ -73,31 +81,71 @@
                 t = jnp.where(low32, -t, t)
             ref[b * BLK:(b + 1) * BLK, :] = t
 
-    pl.semaphore_wait(barrier, 7)
-
-    def slot(j, l):
-        return wo_all.at[j, pl.ds(l * 64, 64)]
-
-    for k, j in enumerate(order):
-        rcopy(wo_ref.at[pl.ds(lane * 64, 64)], slot(tp, lane), wz_ss.at[k], w_rs.at[tp, lane], (dp, j, cp)).start()
-
-    def wz(k):
-        return rcopy(slot(order[k], lane), slot(order[k], lane), wz_ss.at[k], w_rs.at[order[k], lane], (dp, order[k], cp))
-
-    def wsend(k, i, l, dev):
-        return rcopy(slot(order[k], l), slot(order[k], l), w_ss.at[k, i], w_rs.at[order[k], l], dev)
-
-    def wforward(k, i, l):
-        return rcopy(slot(order[k], l), slot(order[k], l), f_ss.at[k, i], w_rs.at[order[k], l], partner)
-
-    def w_arrive(k):
-        wz(k).wait_recv()
-        for i, dev in enumerate(peers + (partner,)):
-            wsend(k, i, lane, dev).start()
+    pl.semaphore_wait(barrier, 5 + mid)
+
+    def slot(j, l, half):
+        return wo_all.at[j, pl.ds(l * 64 + half * 32, 32)]
+
+    def wz(direction, j, half):
+        part = slot(j, lane, half)
+        return rcopy(part, part, wz_ss.at[direction, j, half], w_rs.at[j, lane, half], right if direction == 0 else left)
+
+    def wsend(j, half, i, l, dev):
+        part = slot(j, l, half)
+        return rcopy(part, part, w_ss.at[j, half, i], w_rs.at[j, l, half], dev)
+
+    def wforward(j, half, i, l):
+        part = slot(j, l, half)
+        return rcopy(part, part, f_ss.at[j, half, i], w_rs.at[j, l, half], partner)
+
+    def wz_step(s, half):
+        @pl.when(tp >= s)
+        def _():
+            wz(0, tp - s, half).wait_recv()
+
+        @pl.when((tp >= s) & (tp < TP - 1))
+        def _():
+            wz(0, tp - s, half).start()
+
+        @pl.when(tp >= s)
+        def _():
+            for i, dev in enumerate(peers + (partner,)):
+                wsend(tp - s, half, i, lane, dev).start()
+
+        @pl.when(tp + s < TP)
+        def _():
+            wz(1, tp + s, half).wait_recv()
+
+        @pl.when((tp + s < TP) & (tp > 0))
+        def _():
+            wz(1, tp + s, half).start()
+
+        @pl.when(tp + s < TP)
+        def _():
+            for i, dev in enumerate(peers + (partner,)):
+                wsend(tp + s, half, i, lane, dev).start()
+
+    loads[5].wait()
+
+    @pl.when(tp < TP - 1)
+    def _():
+        wz(0, tp, 0).start()
+        wz(0, tp, 1).start()
+
+    @pl.when(tp > 0)
+    def _():
+        wz(1, tp, 0).start()
+        wz(1, tp, 1).start()
 
     def w_step(k, i):
-        wsend(k, i, lanes[i], peers[i]).wait_recv()
-        wforward(k, i, lanes[i]).start()
+        for half in range(2):
+            wsend(order[k], half, i, lanes[i], peers[i]).wait_recv()
+            wforward(order[k], half, i, lanes[i]).start()
+
+    def w_ready(k):
+        for l in p_lanes:
+            for half in range(2):
+                wforward(order[k], half, 0, l).wait_recv()
 
     def norm(b):
         rows = pl.ds(b * PIECE, PIECE)
@@ -148,28 +196,37 @@
             qm[g // 2, b, at:at + PIECE, :] = jnp.where(low_head, q, zero)
             qm[g // 2, b, at + PIECE:at + 2 * PIECE, :] = jnp.where(low_head, zero, q)
 
-    w_arrive(0)
-    for b in range(2):
-        kvc(0, b, nb[b], ynb).wait_recv()
-        kvc(2, b, nb[b], partner).start()
-    for b in range(2):
-        kvc(1, b, pt[b], partner).wait_recv()
-        kvc(2, b, pd[b], partner).wait_recv()
-
-    def double(piece, carry):
+    def double(piece):
         for i, ref in enumerate((kk, vv)):
             t = kv_all[piece, :, i * 128:(i + 1) * 128]
             r = pltpu.roll(t.astype(F32), 64, 1).astype(BF16)
             ref[0, piece] = jnp.where(low_head, t, r)
             ref[1, piece] = jnp.where(low_head, r, t)
-        return carry
-
-    lax.fori_loop(0, 8, double, 0)
+
+    wz_step(1, 0)
+    double(mine[0])
+    double(mine[1])
+    kvc(0, 0, nb[0], ynb).wait_recv()
+    kvc(2, 0, nb[0], partner).start()
+    double(nb[0])
+    wz_step(1, 1)
+    kvc(1, 0, pt[0], partner).wait_recv()
+    double(pt[0])
+    kvc(1, 1, pt[1], partner).wait_recv()
+    double(pt[1])
+    kvc(0, 1, nb[1], ynb).wait_recv()
+    kvc(2, 1, nb[1], partner).start()
+    double(nb[1])
+    kvc(2, 0, pd[0], partner).wait_recv()
+    double(pd[0])
+    kvc(2, 1, pd[1], partner).wait_recv()
+    double(pd[1])
+    wz_step(2, 0)
 
     q_iota = lax.broadcasted_iota(jnp.int32, (PIECE, PIECE), 0)
     k_iota = lax.broadcasted_iota(jnp.int32, (PIECE, PIECE), 1)
 
-    def attend(n, b):
+    def attend(n, b, poll):
         piece = mine[b]
         pos_c = jnp.concatenate([pos_t[:, 2 * b:2 * b + 1], pos_t[:, 2 * b + 1:2 * b + 2]], axis=0).astype(jnp.int32)
         start_c = q_iota[:, 0:1] - pos_c
@@ -188,6 +245,7 @@
             return carry
 
         lax.fori_loop(0, piece + 1, score, 0)
+        poll()
         m_s[...] = jnp.broadcast_to(jnp.max(m_s[...], axis=-1, keepdims=True), m_s.shape)
 
         def expo(kp, carry):
@@ -220,79 +278,109 @@
         part = o_all.at[src, sub // 2, pl.ds((sub % 2) * PIECE, PIECE)]
         return rcopy(part, part, o_ss.at[direction, src, sub], o_rs.at[src, sub], right if direction == 0 else left)
 
-    for n in range(2):
-        for b in range(2):
-            attend(n, b)
-            sub = 2 * n + b
-
-            @pl.when(tp < TP - 1)
-            def _():
-                oc(0, tp, sub).start()
-
-            @pl.when(tp > 0)
-            def _():
-                oc(1, tp, sub).start()
-
-            if sub < 2:
-                w_arrive(sub + 1)
-
-    def product(j, rows, last):
+    def o_step(s, sub):
+        @pl.when(tp >= s)
+        def _():
+            oc(0, tp - s, sub).wait_recv()
+
+        @pl.when((tp >= s) & (tp < TP - 1))
+        def _():
+            oc(0, tp - s, sub).start()
+
+        @pl.when(tp + s < TP)
+        def _():
+            oc(1, tp + s, sub).wait_recv()
+
+        @pl.when((tp + s < TP) & (tp > 0))
+        def _():
+            oc(1, tp + s, sub).start()
+
+    def o_send(sub):
+        @pl.when(tp < TP - 1)
+        def _():
+            oc(0, tp, sub).start()
+
+        @pl.when(tp > 0)
+        def _():
+            oc(1, tp, sub).start()
+
+    def nothing():
+        pass
+
+    attend(0, 0, lambda: wz_step(2, 1))
+    o_send(0)
+    attend(0, 1, nothing)
+    o_send(1)
+    wz_step(3, 0)
+    wz_step(3, 1)
+    attend(1, 0, nothing)
+    o_send(2)
+    o_step(1, 0)
+    attend(1, 1, lambda: o_step(1, 1))
+    o_send(3)
+
+    def product(j):
         for t in range(4):
             cols = slice(t * 512, (t + 1) * 512)
-            part = jnp.dot(o_all[j, 0, rows, :], wo_all[j, 0:256, cols], preferred_element_type=F32)
-            part += jnp.dot(o_all[j, 1, rows, :], wo_all[j, 256:512, cols], preferred_element_type=F32)
-            if last:
-                y_ref[rows, cols] = (acc[rows, cols] + part).astype(BF16)
-            else:
-                acc[rows, cols] += part
-
-    every = slice(0, ROWS)
-    loads[5].wait()
+            part = jnp.dot(o_all[j, 0], wo_all[j, 0:256, cols], preferred_element_type=F32)
+            part += jnp.dot(o_all[j, 1], wo_all[j, 256:512, cols], preferred_element_type=F32)
+            acc[:, cols] += part
+
     for t in range(4):
         cols = slice(t * 512, (t + 1) * 512)
         acc[:, cols] = xv[:, cols].astype(F32)
-    product(tp, every, False)
-
-    def o_step(s, sub):
-        @pl.when(tp >= s)
-        def _():
-            oc(0, tp - s, sub).wait_recv()
-
-        @pl.when((tp >= s) & (tp < TP - 1))
-        def _():
-            oc(0, tp - s, sub).start()
-
-        @pl.when(tp + s < TP)
-        def _():
-            oc(1, tp + s, sub).wait_recv()
-
-        @pl.when((tp + s < TP) & (tp > 0))
-        def _():
-            oc(1, tp + s, sub).start()
-
-    for k in range(3):
-        s = k + 1
-        o_step(s, 0)
-        w_step(k, 0)
-        o_step(s, 1)
-        w_step(k, 1)
-        o_step(s, 2)
-        w_step(k, 2)
-        o_step(s, 3)
-        for l in p_lanes:
-            wforward(k, 0, l).wait_recv()
-        product(order[k], every, k == 2)
+    product(tp)
+
+    for i in range(3):
+        w_step(0, i)
+    o_step(1, 2)
+    o_step(1, 3)
+    w_ready(0)
+    product(order[0])
+    o_step(2, 0)
+    o_step(2, 1)
+    for i in range(3):
+        w_step(1, i)
+    o_step(2, 2)
+    o_step(2, 3)
+    w_ready(1)
+    product(order[1])
+    for i in range(3):
+        w_step(2, i)
+    o_step(3, 0)
+    w_ready(2)
+    for sub in range(4):
+        n, b = sub // 2, sub % 2
+        rows = slice(b * PIECE, (b + 1) * PIECE)
+        if sub > 0:
+            o_step(3, sub)
+        for t in range(4):
+            cols = slice(t * 512, (t + 1) * 512)
+            part = jnp.dot(o_all[order[2], n, rows, :], wo_all[order[2], n * 256:(n + 1) * 256, cols], preferred_element_type=F32)
+            if n == 0:
+                acc[rows, cols] += part
+            else:
+                y_ref[rows, cols] = (acc[rows, cols] + part).astype(BF16)
 
     for b in range(2):
         kvc(0, b, mine[b], ynb).wait_send()
         kvc(1, b, mine[b], partner).wait_send()
         kvc(2, b, nb[b], partner).wait_send()
-    for k in range(3):
-        wz(k).wait_send()
-        for i, dev in enumerate(peers + (partner,)):
-            wsend(k, i, lane, dev).wait_send()
-        for i in range(3):
-            wforward(k, i, lanes[i]).wait_send()
+    for j in order:
+        for half in range(2):
+            for i, dev in enumerate(peers + (partner,)):
+                wsend(j, half, i, lane, dev).wait_send()
+            for i in range(3):
+                wforward(j, half, i, lanes[i]).wait_send()
+    for s in range(0, TP):
+        for half in range(2):
+            @pl.when((tp >= s) & (tp < TP - 1))
+            def _():
+                wz(0, tp - s, half).wait_send()
+
+            @pl.when((tp + s < TP) & (tp > 0))
+            def _():
+                wz(1, tp + s, half).wait_send()
     for s in range(0, TP):
         for sub in range(4):
             @pl.when((tp >= s) & (tp < TP - 1))
@@ -306,11 +394,10 @@
 
 def layer(x, pos, gain, freq, wq, wk, wv, wo):
     hbm, vm = pl.BlockSpec(memory_space=pltpu.HBM), pl.BlockSpec(memory_space=pltpu.VMEM)
-    sds = jax.ShapeDtypeStruct
     dma = pltpu.SemaphoreType.DMA
     return pl.pallas_call(
         layer_kernel,
-        out_shape=(sds((ROWS, DM), BF16), sds((128, ROWS), BF16), sds((128, ROWS), BF16)),
+        out_shape=(pltpu.VMEM((ROWS, DM), BF16), pltpu.VMEM((128, ROWS), BF16), pltpu.VMEM((128, ROWS), BF16)),
         in_specs=[hbm, vm, vm, vm, hbm, hbm, hbm, hbm],
         out_specs=(vm, vm, vm),
         scratch_shapes=[
@@ -320,7 +407,7 @@
             pltpu.VMEM((8, 4 * PIECE, PIECE), F32),
             pltpu.VMEM((4 * PIECE, 128), F32), pltpu.VMEM((4 * PIECE, 128), F32), pltpu.VMEM((4 * PIECE, 128), F32),
             pltpu.VMEM((TP, 2, ROWS, 256), BF16), pltpu.VMEM((TP, 512, DM), BF16), pltpu.VMEM((ROWS, DM), F32),
-            dma((6,)), dma((3, 2)), dma((3, 2)), dma((3,)), dma((3, 4)), dma((3, 3)), dma((TP, 8)), dma((2, TP, 4)), dma((TP, 4)),
+            dma((6,)), dma((3, 2)), dma((3, 2)), dma((2, TP, 2)), dma((TP, 2, 4)), dma((TP, 2, 3)), dma((TP, 8, 2)), dma((2, TP, 4)), dma((TP, 4)),
         ],
         compiler_params=pltpu.CompilerParams(collective_id=0, has_side_effects=True, vmem_limit_bytes=60 * 1024 * 1024),
         name='layer',

time: 77.7 us -> 64.4 us (0.83)
  Pallas kernels: 72.3 us -> 60.9 us
  local copies, waits for them, and re-layouts: 4.52 us -> 2.63 us
    pallas_call x1, Pallas kernels: 72.3 us -> 60.9 us  [layer(): pl.pallas_call(layer_kernel, out_shape=(pltpu.VMEM((ROWS, DM), BF16), plt...]
    unnamed x7 -> x3, local copies, waits for them, and re-layouts: 4.52 us -> 2.63 us
where the time goes in v3:
time: 64.4 us; the launch traced here: 64.2 us
  Pallas kernels  60.9 us (95%)
  local copies, waits for them, and re-layouts  2.63 us (4%)
    pallas_call x1, Pallas kernels, layer(): pl.pallas_call(layer_kernel, out_shape=(pltpu.VMEM((ROWS, DM), BF16), plt...  60.9 us
    unnamed x3, local copies, waits for them, and re-layouts  2.63 us

profile of v3, /device:TPU:0, one launch (start us, length us, event | category | flops | bytes accessed | tf_op | source)
XLA Modules:
  0.0 64.2 jit_solution(11833524136085647471)
XLA Ops:
  0.6 60.9 %layer.1 = (bf16[512,2048]{1,0:T(8,128)(2,1)S(1)}, bf16[128,512]{1,0:T(8,128)(2,1)S(1)}, bf16[128,512]{1,0:T(8,128)(2,1)S(1)}) custom-call(bf16[512,2048]{1,0:T(8,128)(2,1)} %x_ref.1, s32[4,128]{1,0:T(4,128)} %bitcast.12, f32[1,2048]{1,0:T(1,128)} %bitcast.11, f32[1,32]{1,0:T(1,128)} %bitcast.13, bf16[2048,512]{1,0:T(8,128)(2,1)} %wq_ref.1, ...), custom_call_target="tpu_custom_call" | custom-call | tf_op jit(solution)/shard_map/layer/pallas_call | solution.py:398
  61.6 1.3 %copy.14 = bf16[512,2048]{1,0:T(8,128)(2,1)} copy(bf16[512,2048]{1,0:T(8,128)(2,1)S(1)} %get-tuple-element.9) | data formatting | bytes 4194304
  62.9 0.7 %copy.15 = bf16[512,2,64]{0,2,1:T(8,128)(2,1)} copy(bf16[512,2,64]{0,2,1:T(8,128)(2,1)S(1)} %bitcast.10) | data formatting | bytes 262144
  63.6 0.7 %copy.16 = bf16[512,2,64]{0,2,1:T(8,128)(2,1)} copy(bf16[512,2,64]{0,2,1:T(8,128)(2,1)S(1)} %bitcast.9) | data formatting | bytes 262144

commit v4 on v3

--- a/solution.py
+++ b/solution.py
@@ -21,8 +21,8 @@
 
 
 def layer_kernel(x_ref, pos_ref, gain_ref, freq_ref, wq_ref, wk_ref, wv_ref, wo_ref,
-                 y_ref, kt_ref, vt_ref,
-                 xv, wqv, wkv, h, cosv, sinv, kv_all, kk, vv, qm, st, m_s, l_s, a_s, o_all, wo_all, acc,
+                 ya_ref, accb_ref, olast_ref, wlast_ref, kt_ref, vt_ref,
+                 posv, gainv, freqv, xv, wqv, wkv, h, cosv, sinv, kv_all, kk, vv, qm, st, m_s, l_s, a_s, o_all, wo_all, acca,
                  lsem, kv_ss, kv_rs, wz_ss, w_ss, f_ss, w_rs, o_ss, o_rs):
     dp, tp, cp = lax.axis_index('dp'), lax.axis_index('tp'), lax.axis_index('cp')
     y, c = cp // 2, cp % 2
@@ -60,12 +60,16 @@
     loads.append(pltpu.make_async_copy(wv_ref, wkv.at[:, pl.ds(128, 128)], lsem.at[3]))
     loads.append(pltpu.make_async_copy(wq_ref, wqv, lsem.at[4]))
     loads.append(pltpu.make_async_copy(wo_ref, wo_all.at[tp], lsem.at[5]))
-    for i in (5, 0, 2, 3, 1, 4):
+    for i, (src, dst) in enumerate(((pos_ref, posv), (freq_ref, freqv), (gain_ref, gainv))):
+        loads.append(pltpu.make_async_copy(src, dst, lsem.at[6 + i]))
+    for i in (6, 7, 5, 8, 0, 2, 3, 1, 4):
         loads[i].start()
+    loads[6].wait()
+    loads[7].wait()
 
     lane_i = lax.broadcasted_iota(jnp.int32, (BLK, 128), 1)
-    pos_t = jnp.concatenate([pos_ref[...].astype(F32), jnp.zeros((4, BLK), F32)], axis=0).T
-    freq = jnp.concatenate([freq_ref[...]] * 4, axis=1)
+    pos_t = jnp.concatenate([posv[...].astype(F32), jnp.zeros((4, BLK), F32)], axis=0).T
+    freq = jnp.concatenate([freqv[...]] * 4, axis=1)
     pos_l = jnp.zeros((BLK, 128), F32)
     for b in range(4):
         pos_l = jnp.where(lane_i // 32 == b, pos_t[:, b:b + 1], pos_l)
@@ -151,7 +155,7 @@
         rows = pl.ds(b * PIECE, PIECE)
         xf = xv[rows, :].astype(F32)
         inv = lax.rsqrt(jnp.mean(xf * xf, axis=-1, keepdims=True) + 1e-5)
-        h[rows, :] = (xf * inv * gain_ref[...]).astype(BF16)
+        h[rows, :] = (xf * inv * gainv[...]).astype(BF16)
 
     low = lax.broadcasted_iota(jnp.int32, (PIECE, 128), 1)
     low_head = low < 64
@@ -170,6 +174,8 @@
 
     for b in range(2):
         rows = slice(b * PIECE, (b + 1) * PIECE)
+        if b == 0:
+            loads[8].wait()
         loads[b].wait()
         norm(b)
         if b == 0:
@@ -226,7 +232,7 @@
     q_iota = lax.broadcasted_iota(jnp.int32, (PIECE, PIECE), 0)
     k_iota = lax.broadcasted_iota(jnp.int32, (PIECE, PIECE), 1)
 
-    def attend(n, b, poll):
+    def attend(n, b, poll, poll2=lambda: None):
         piece = mine[b]
         pos_c = jnp.concatenate([pos_t[:, 2 * b:2 * b + 1], pos_t[:, 2 * b + 1:2 * b + 2]], axis=0).astype(jnp.int32)
         start_c = q_iota[:, 0:1] - pos_c
@@ -259,6 +265,7 @@
             return carry
 
         lax.fori_loop(0, piece + 1, expo, 0)
+        poll2()
         l_s[...] = jnp.broadcast_to(1.0 / jnp.sum(l_s[...], axis=-1, keepdims=True), l_s.shape)
 
         def mix(kp, carry):
@@ -275,7 +282,7 @@
             o_all[tp, n, b * PIECE:(b + 1) * PIECE, a * 128:(a + 1) * 128] = jnp.where(low_head, even, odd).astype(BF16)
 
     def oc(direction, src, sub):
-        part = o_all.at[src, sub // 2, pl.ds((sub % 2) * PIECE, PIECE)]
+        part = o_all.at[src, sub % 2, pl.ds((sub // 2) * PIECE, PIECE)]
         return rcopy(part, part, o_ss.at[direction, src, sub], o_rs.at[src, sub], right if direction == 0 else left)
 
     def o_step(s, sub):
@@ -307,28 +314,31 @@
     def nothing():
         pass
 
-    attend(0, 0, lambda: wz_step(2, 1))
+    attend(0, 0, nothing, lambda: wz_step(2, 1))
     o_send(0)
-    attend(0, 1, nothing)
+    attend(1, 0, nothing)
     o_send(1)
     wz_step(3, 0)
-    wz_step(3, 1)
-    attend(1, 0, nothing)
+    attend(0, 1, nothing, lambda: wz_step(3, 1))
     o_send(2)
-    o_step(1, 0)
-    attend(1, 1, lambda: o_step(1, 1))
+    attend(1, 1, lambda: o_step(1, 0))
     o_send(3)
+    o_step(1, 1)
+
+    accs = (acca, accb_ref)
 
     def product(j):
-        for t in range(4):
-            cols = slice(t * 512, (t + 1) * 512)
-            part = jnp.dot(o_all[j, 0], wo_all[j, 0:256, cols], preferred_element_type=F32)
-            part += jnp.dot(o_all[j, 1], wo_all[j, 256:512, cols], preferred_element_type=F32)
-            acc[:, cols] += part
-
-    for t in range(4):
-        cols = slice(t * 512, (t + 1) * 512)
-        acc[:, cols] = xv[:, cols].astype(F32)
+        for b in range(2):
+            rows = slice(b * PIECE, (b + 1) * PIECE)
+            for t in range(4):
+                cols = slice(t * 512, (t + 1) * 512)
+                part = jnp.dot(o_all[j, 0, rows, :], wo_all[j, 0:256, cols], preferred_element_type=F32)
+                part += jnp.dot(o_all[j, 1, rows, :], wo_all[j, 256:512, cols], preferred_element_type=F32)
+                accs[b][:, cols] += part
+
+    for b in range(2):
+        rows = slice(b * PIECE, (b + 1) * PIECE)
+        accs[b][...] = xv[rows, :].astype(F32)
     product(tp)
 
     for i in range(3):
@@ -349,18 +359,19 @@
         w_step(2, i)
     o_step(3, 0)
     w_ready(2)
-    for sub in range(4):
-        n, b = sub // 2, sub % 2
-        rows = slice(b * PIECE, (b + 1) * PIECE)
-        if sub > 0:
-            o_step(3, sub)
-        for t in range(4):
-            cols = slice(t * 512, (t + 1) * 512)
-            part = jnp.dot(o_all[order[2], n, rows, :], wo_all[order[2], n * 256:(n + 1) * 256, cols], preferred_element_type=F32)
-            if n == 0:
-                acc[rows, cols] += part
-            else:
-                y_ref[rows, cols] = (acc[rows, cols] + part).astype(BF16)
+    far = order[2]
+    w_out = pltpu.make_async_copy(wo_all.at[far, pl.ds(256, 256)], wlast_ref, lsem.at[9])
+    w_out.start()
+    o_step(3, 1)
+    for t in range(4):
+        cols = slice(t * 512, (t + 1) * 512)
+        part = jnp.dot(o_all[far, 0, 0:PIECE, :], wo_all[far, 0:256, cols], preferred_element_type=F32)
+        part += jnp.dot(o_all[far, 1, 0:PIECE, :], wo_all[far, 256:512, cols], preferred_element_type=F32)
+        ya_ref[:, cols] = (acca[:, cols] + part).astype(BF16)
+    o_step(3, 2)
+    for t in range(4):
+        cols = slice(t * 512, (t + 1) * 512)
+        accb_ref[:, cols] += jnp.dot(o_all[far, 0, PIECE:ROWS, :], wo_all[far, 0:256, cols], preferred_element_type=F32)
 
     for b in range(2):
         kvc(0, b, mine[b], ynb).wait_send()
@@ -390,6 +401,9 @@
             @pl.when((tp + s < TP) & (tp > 0))
             def _():
                 oc(1, tp + s, sub).wait_send()
+    w_out.wait()
+    o_step(3, 3)
+    olast_ref[...] = o_all[far, 1, PIECE:ROWS, :]
 
 
 def layer(x, pos, gain, freq, wq, wk, wv, wo):
@@ -397,26 +411,59 @@
     dma = pltpu.SemaphoreType.DMA
     return pl.pallas_call(
         layer_kernel,
-        out_shape=(pltpu.VMEM((ROWS, DM), BF16), pltpu.VMEM((128, ROWS), BF16), pltpu.VMEM((128, ROWS), BF16)),
-        in_specs=[hbm, vm, vm, vm, hbm, hbm, hbm, hbm],
-        out_specs=(vm, vm, vm),
+        out_shape=(pltpu.VMEM((PIECE, DM), BF16), pltpu.VMEM((PIECE, DM), F32), pltpu.VMEM((PIECE, 256), BF16), pltpu.VMEM((256, DM), BF16), pltpu.VMEM((128, ROWS), BF16), pltpu.VMEM((128, ROWS), BF16)),
+        in_specs=[hbm] * 8,
+        out_specs=(vm,) * 6,
         scratch_shapes=[
+            pltpu.VMEM((4, BLK), jnp.int32), pltpu.VMEM((1, DM), F32), pltpu.VMEM((1, 32), F32),
             pltpu.VMEM((ROWS, DM), BF16), pltpu.VMEM((DM, 512), BF16), pltpu.VMEM((DM, 256), BF16), pltpu.VMEM((ROWS, DM), BF16),
             pltpu.VMEM((ROWS, 128), F32), pltpu.VMEM((ROWS, 128), F32), pltpu.VMEM((8, PIECE, 256), BF16),
             pltpu.VMEM((2, 8, PIECE, 128), BF16), pltpu.VMEM((2, 8, PIECE, 128), BF16), pltpu.VMEM((2, 2, 4 * PIECE, 128), BF16),
             pltpu.VMEM((8, 4 * PIECE, PIECE), F32),
             pltpu.VMEM((4 * PIECE, 128), F32), pltpu.VMEM((4 * PIECE, 128), F32), pltpu.VMEM((4 * PIECE, 128), F32),
-            pltpu.VMEM((TP, 2, ROWS, 256), BF16), pltpu.VMEM((TP, 512, DM), BF16), pltpu.VMEM((ROWS, DM), F32),
-            dma((6,)), dma((3, 2)), dma((3, 2)), dma((2, TP, 2)), dma((TP, 2, 4)), dma((TP, 2, 3)), dma((TP, 8, 2)), dma((2, TP, 4)), dma((TP, 4)),
+            pltpu.VMEM((TP, 2, ROWS, 256), BF16), pltpu.VMEM((TP, 512, DM), BF16), pltpu.VMEM((PIECE, DM), F32),
+            dma((10,)), dma((3, 2)), dma((3, 2)), dma((2, TP, 2)), dma((TP, 2, 4)), dma((TP, 2, 3)), dma((TP, 8, 2)), dma((2, TP, 4)), dma((TP, 4)),
         ],
-        compiler_params=pltpu.CompilerParams(collective_id=0, has_side_effects=True, vmem_limit_bytes=60 * 1024 * 1024),
+        compiler_params=pltpu.CompilerParams(collective_id=0, has_side_effects=True, vmem_limit_bytes=58 * 1024 * 1024),
         name='layer',
     )(x, pos, gain, freq, wq, wk, wv, wo)
 
 
+def finish_kernel(ya_ref, accb_ref, olast_ref, wlast_ref, kt_ref, vt_ref, y_out, kt_out, vt_out, yb, sem):
+    copies = []
+
+    def put(src, dst, i):
+        copies.append(pltpu.make_async_copy(src, dst, sem.at[i]))
+        copies[-1].start()
+
+    put(ya_ref, y_out.at[pl.ds(0, PIECE)], 0)
+    put(kt_ref, kt_out, 1)
+    put(vt_ref, vt_out, 2)
+    for t in range(4):
+        cols = slice(t * 512, (t + 1) * 512)
+        part = jnp.dot(olast_ref[...], wlast_ref[:, cols], preferred_element_type=F32)
+        yb[:, cols] = (accb_ref[:, cols] + part).astype(BF16)
+        put(yb.at[:, pl.ds(t * 512, 512)], y_out.at[pl.ds(PIECE, PIECE), pl.ds(t * 512, 512)], 3 + t)
+    for cpy in copies:
+        cpy.wait()
+
+
+def finish(*parts):
+    sds = jax.ShapeDtypeStruct
+    return pl.pallas_call(
+        finish_kernel,
+        out_shape=(sds((ROWS, DM), BF16), sds((128, ROWS), BF16), sds((128, ROWS), BF16)),
+        in_specs=[pl.BlockSpec(memory_space=pltpu.VMEM)] * 6,
+        out_specs=(pl.BlockSpec(memory_space=pltpu.HBM),) * 3,
+        scratch_shapes=[pltpu.VMEM((PIECE, DM), BF16), pltpu.SemaphoreType.DMA((7,))],
+        compiler_params=pltpu.CompilerParams(vmem_limit_bytes=8 * 1024 * 1024),
+        name='finish',
+    )(*parts)
+
+
 def solution(mesh):
     def local_step(x, doc_id, pos, gain, wq, wk, wv, wo, inv_freq):
-        y, kt, vt = layer(x, pos.reshape(4, BLK), gain.reshape(1, DM), inv_freq.reshape(1, 32), wq, wk, wv, wo)
+        y, kt, vt = finish(*layer(x, pos.reshape(4, BLK), gain.reshape(1, DM), inv_freq.reshape(1, 32), wq, wk, wv, wo))
         return y, kt.T.reshape(ROWS, 2, 64), vt.T.reshape(ROWS, 2, 64)
 
     row_spec = P(('dp', 'cp'))

time: 64.4 us -> 62.9 us (0.977)
  local copies, waits for them, and re-layouts: 2.63 us -> 0 us
  Pallas kernels: 60.9 us -> 61.9 us
    unnamed x3 -> x0, local copies, waits for them, and re-layouts: 2.63 us -> none
    pallas_call x1 -> x2, Pallas kernels: 60.9 us -> 61.9 us  [the longest x1 60.5 us: layer(): pl.pallas_call(layer_kernel, out_shape=(pltpu.VMEM((PIECE, DM), BF16), pl...]
where the time goes in v4:
time: 62.9 us; the launch traced here: 62.7 us
  Pallas kernels  61.9 us (98%)
  between operations  0.8 us (1%)
    pallas_call x1, Pallas kernels, layer(): pl.pallas_call(layer_kernel, out_shape=(pltpu.VMEM((PIECE, DM), BF16), pl...  60.5 us
    pallas_call x1, Pallas kernels, finish(): pl.pallas_call(finish_kernel, out_shape=(sds((ROWS, DM), BF16), sds((128,...  1.46 us

profile of v4, /device:TPU:0, one launch (start us, length us, event | category | flops | bytes accessed | tf_op | source)
XLA Modules:
  0.0 62.7 jit_solution(16260104306635875086)
XLA Ops:
  0.6 60.5 %layer.1 = (bf16[256,2048]{1,0:T(8,128)(2,1)S(1)}, f32[256,2048]{1,0:T(8,128)S(1)}, bf16[256,256]{1,0:T(8,128)(2,1)S(1)}, bf16[256,2048]{1,0:T(8,128)(2,1)S(1)},...) custom-call(bf16[512,2048]{1,0:T(8,128)(2,1)} %x_ref.1, s32[4,128]{1,0:T(4,128)} %bitcast.10, ...), custom_call_target="tpu_custom_call" | custom-call | tf_op jit(solution)/shard_map/layer/pallas_call | solution.py:412
  61.1 1.5 %finish.1 = (bf16[512,2048]{1,0:T(8,128)(2,1)}, bf16[128,512]{1,0:T(8,128)(2,1)}, bf16[128,512]{1,0:T(8,128)(2,1)}) custom-call(bf16[256,2048]{1,0:T(8,128)(2,1)S(1)} %get-tuple-element.12.ya_ref, f32[256,2048]{1,0:T(8,128)S(1)} %get-tuple-element.13.accb_ref, bf16[256,256]{1,0:T(8,128)(2,1)S(1)} %get-tuple-element.14.olast_ref, ...), custom_call_target="tpu_custom_call" | custom-call | tf_op jit(solution)/shard_map/finish/pallas_call | solution.py:453
